TPU v7x, 16 devices: a whole 2x2x2 slice. The times are simulated.
16 devices in a mesh: rep: 1, r: 4 (over y, z), s: 4 (over x, core).
Axes of the slice: x: 2, y: 2, z: 2, core: 2. Of those that a mesh axis runs over, the one named last changes fastest.
Arguments:
- x: bfloat16 [16, 4096, 896], P(('rep', 'r', 's'))
- dy: bfloat16 [16, 4096, 896], P(('rep', 'r', 's'))
- w_gate: bfloat16 [2, 896, 2560], P(None, 's')
- w_up: bfloat16 [2, 896, 2560], P(None, 's')
- w_down: bfloat16 [2, 2560, 896], P(None, 's')
- m_w_gate: float32 [2, 896, 2560], P(None, 's')
- m_w_up: float32 [2, 896, 2560], P(None, 's')
- m_w_down: float32 [2, 2560, 896], P(None, 's')
- v_w_gate: float32 [2, 896, 2560], P(None, 's')
- v_w_up: float32 [2, 896, 2560], P(None, 's')
- v_w_down: float32 [2, 2560, 896], P(None, 's')
Outputs:
- output 1: bfloat16 [2, 896, 2560], P('rep', 's')
- output 2: bfloat16 [2, 896, 2560], P('rep', 's')
- output 3: bfloat16 [2, 2560, 896], P('rep', 's')
- output 4: float32 [2, 896, 2560], P('rep', 's')
- output 5: float32 [2, 896, 2560], P('rep', 's')
- output 6: float32 [2, 2560, 896], P('rep', 's')
- output 7: float32 [2, 896, 2560], P('rep', 's')
- output 8: float32 [2, 896, 2560], P('rep', 's')
- output 9: float32 [2, 2560, 896], P('rep', 's')
All inputs are finite; a program needn't handle non-finite values.
Results may differ from a plain program's by a relative error of at most 0.022.
Values are sent between devices in bfloat16 or wider.
A program may use at most 2 GiB of HBM per device.

v0:
```python
import jax
import jax.numpy as jnp
from jax import lax
from jax.sharding import PartitionSpec as P

NAMES = ("w_gate", "w_up", "w_down")


def matmul(a, w):
    return jnp.dot(a, w, preferred_element_type=jnp.float32).astype(jnp.bfloat16)


def normed(h):
    wide = h.astype(jnp.float32)
    scale = lax.rsqrt(jnp.mean(wide**2, -1, keepdims=True) + 1e-6)
    return (wide * scale).astype(jnp.bfloat16)


def layer(h, w):
    a = normed(h)
    gate = jnp.dot(a, w["w_gate"], preferred_element_type=jnp.float32)
    up = jnp.dot(a, w["w_up"], preferred_element_type=jnp.float32)
    return h + matmul((jax.nn.silu(gate) * up).astype(jnp.bfloat16), w["w_down"])


def adamw(w, m, v, g):
    m = 0.9 * m + 0.1 * g
    v = 0.95 * v + 0.05 * g * g
    step = m * lax.rsqrt(v + 1e-8) + 0.1 * w
    return (w - 0.02 * step).astype(jnp.bfloat16), m, v


def clipped(gradients, sum_of_squares, count):
    factor = jnp.minimum(1.0, 0.5 * lax.rsqrt(sum_of_squares / count + 1e-30))
    return [g * factor for g in gradients]


def solution(mesh):
    def fetched(weights, number):
        return {name: lax.all_gather(w[number], "s", axis=0, tiled=True) for name, w in zip(NAMES, weights, strict=True)}

    def summed(term):
        return lax.psum(lax.psum_scatter(term, "s", scatter_dimension=0, tiled=True), "r")

    def step(x, dy, *arrays):
        weights, m, v = (arrays[i : i + 3] for i in (0, 3, 6))
        layers = weights[0].shape[0]
        h, kept = x[0], []
        for number in range(layers):
            kept.append(h)
            h = layer(h, fetched(weights, number))
        by_h, mine = dy[0], [None] * layers
        for number in reversed(range(layers)):
            _, back = jax.vjp(lambda w, h: layer(h, w), fetched(weights, number), kept[number])
            by_w, by_h = back(by_h)
            mine[number] = [summed(by_w[name]) for name in NAMES]
        gradients = [jnp.stack([mine[number][i] for number in range(layers)]).astype(jnp.float32) for i in range(3)]
        squares = lax.psum(sum(jnp.sum(g * g) for g in gradients), "s")
        gradients = clipped(gradients, squares, lax.psum(1, "s") * sum(g.size for g in gradients))
        new = [adamw(w.astype(jnp.float32), m, v, g) for w, m, v, g in zip(weights, m, v, gradients, strict=True)]
        return tuple(one[which] for which in range(3) for one in new)

    states, cut = P(("rep", "r", "s"), None, None), P(None, "s", None)
    return jax.shard_map(
        step,
        mesh=mesh,
        in_specs=(states, states) + (cut,) * 9,
        out_specs=(P("rep", "s", None),) * 9,
        check_vma=False,
    )
```

profile of v0, /device:TPU:0, one launch (start us, length us, event | category | flops | bytes accessed | tf_op | source)
XLA Modules:
  0.0 864.7 jit_solution(11402727616073758116)
XLA Ops:
  7.2 3.3 fusion.91
  10.5 0.0 all-gather.15.cloned.1.call-start
  10.6 3.1 fusion.90
  13.8 0.0 all-gather.17.cloned.1.call-start
  13.8 1.6 fusion.89
  15.4 0.5 all-gather.23.cloned.1.call-update
  16.0 0.5 all-gather.21.cloned.1.call-update
  16.6 0.5 all-gather.19.cloned.1.call-update
  17.2 10.8 %copy.20 = bf16[1,4096,896]{1,2,0:T(8,128)(2,1)} copy(bf16[1,4096,896]{2,1,0:T(8,128)(2,1)} %param.11) | data formatting | bytes 14680064 | tf_op args[0]
  28.0 4.6 fusion.15
  32.5 10.7 %copy.21 = bf16[1,4096,896]{1,2,0:T(8,128)(2,1)} copy(bf16[1,4096,896]{2,1,0:T(8,128)(2,1)} %param.12) | data formatting | bytes 14680064 | tf_op args[1]
  43.2 5.0 all-gather.13.cloned.1.call-done
  48.2 29.4 %fusion.47 = f32[4096,2560]{1,0:T(8,128)} fusion(bf16[1,4096,896]{1,2,0:T(8,128)(2,1)} %copy.20, f32[4096]{0:T(1024)S(1)} %add_rsqrt_fusion, bf16[1,896,2560]{2,1,0:T(8,128)(2,1)} %all-gather.13.cloned.1.call-done), kind=kOutput, calls=%fused_computation.72 | convolution fusion | flops 18801491968 | bytes 53886976 | tf_op jit(solution)/shard_map/dot_general | solution.py:21
  77.6 7.4 all-gather.15.cloned.1.call-done
  85.0 49.7 %multiply_convert_fusion.1 = (bf16[4096,2560]{1,0:T(8,128)(2,1)}, f32[4096,2560]{1,0:T(8,128)}) fusion(f32[4096,2560]{1,0:T(8,128)} %fusion.47, bf16[1,896,2560]{2,1,0:T(8,128)(2,1)} %all-gather.15.cloned.1.call-done, bf16[1,4096,896]{1,2,0:T(8,128)(2,1)} %copy.20, f32[4096]{0:T(1024)S(1)} %add_rsqrt_fusion), kind=kOutput, calls=%fused_computation.17 | convolution fusion | flops 18864406528 | bytes 116801536 | tf_op jit(solution)/shard_map/dot_general | solution.py:22
  134.7 26.8 %fusion.19 = (f32[4096]{0:T(1024)S(1)}, bf16[4096,896]{0,1:T(8,128)(2,1)}) fusion(bf16[4096,2560]{1,0:T(8,128)(2,1)} %get-tuple-element.30, bf16[1,2560,896]{2,1,0:T(8,128)(2,1)} %all-gather.17.cloned.1.call-done, bf16[1,4096,896]{1,2,0:T(8,128)(2,1)} %copy.20), kind=kOutput, calls=%fused_computation.37 | convolution fusion | flops 18808827904 | bytes 40255488 | tf_op jit(solution)/shard_map/dot_general | solution.py:10
  161.5 0.6 copy-done.7
  162.2 29.6 %fusion.39 = f32[4096,2560]{1,0:T(8,128)} fusion(bf16[4096,896]{0,1:T(8,128)(2,1)} %get-tuple-element.33, f32[4096]{0:T(1024)S(1)} %fusion.77, bf16[1,896,2560]{2,1,0:T(8,128)(2,1)} %all-gather.23.cloned.1.call-done), kind=kOutput, calls=%fused_computation.69 | convolution fusion | flops 18801491968 | bytes 53886976 | tf_op jit(solution)/shard_map/jvp()/dot_general | solution.py:22
  191.8 3.4 all-gather.21.cloned.1.call-done
  195.2 28.4 %convolution_convert_fusion.1 = bf16[4096,2560]{1,0:T(8,128)(2,1)} fusion(bf16[1,4096,896]{2,1,0:T(8,128)(2,1)} %param.12, bf16[1,2560,896]{2,1,0:T(8,128)(2,1)} %all-gather.21.cloned.1.call-done), kind=kOutput, calls=%fused_computation.27 | convolution fusion | flops 18800967680 | bytes 32899072 | tf_op jit(solution)/shard_map/transpose(jvp())/dot_general | solution.py:10
  223.6 8.3 all-gather.19.cloned.1.call-done
  231.9 58.3 %fusion.2 = (bf16[4096,2560]{1,0:T(8,128)(2,1)}, f32[4096,2560]{1,0:T(8,128)}) fusion(f32[4096,2560]{1,0:T(8,128)} %fusion.39, bf16[4096,2560]{1,0:T(8,128)(2,1)} %convolution_convert_fusion.1, bf16[1,896,2560]{2,1,0:T(8,128)(2,1)} %all-gather.19.cloned.1.call-done, bf16[4096,896]{0,1:T(8,128)(2,1)} %get-tuple-element.33, f32[4096]{0:T(1024)S(1)} %fusion.77), kind=kOutput, calls=%fused_computation.8 | convolution fusion | flops 18927321088 | bytes 137773056 | tf_op jit(solution)/shard_map/jvp()/dot_general | solution.py:21
  290.3 23.6 %fusion.70 = bf16[4096,896]{0,1:T(8,128)(2,1)} fusion(bf16[4096,2560]{1,0:T(8,128)(2,1)} %get-tuple-element.34, bf16[1,896,2560]{2,1,0:T(8,128)(2,1)S(1)} %copy-done.11), kind=kOutput, calls=%fused_computation.94 | convolution fusion | flops 18790481920 | bytes 32899072 | tf_op jit(solution)/shard_map/transpose(jvp())/dot_general | solution.py:21
  313.8 38.7 %fusion.21 = (f32[4096]{0:T(1024)S(1)}, bf16[4096,896]{0,1:T(8,128)(2,1)}) fusion(bf16[4096,896]{0,1:T(8,128)(2,1)} %get-tuple-element.33, bf16[4096,896]{0,1:T(8,128)(2,1)} %fusion.70, bf16[1,896,2560]{2,1,0:T(8,128)(2,1)} %all-gather.23.cloned.1.call-done, bf16[4096,2560]{1,0:T(8,128)(2,1)} %convolution_convert_fusion.1, f32[4096,2560]{1,0:T(8,128)} %get-tuple-element.35), kind=kOutput, calls=%fused_computation.39 | convolution fusion | flops 18875412480 | bytes 89538560 | tf_op jit(solution)/shard_map/transpose(jvp())/dot_general | solution.py:22
  352.6 9.8 %fusion.22 = bf16[4096,896]{0,1:T(8,128)(2,1)S(1)} fusion(bf16[4096,896]{0,1:T(8,128)(2,1)} %get-tuple-element.33, bf16[4096,896]{0,1:T(8,128)(2,1)} %get-tuple-element.37, bf16[1,4096,896]{1,2,0:T(8,128)(2,1)} %copy.21, f32[4096]{0:T(1024)S(1)} %multiply_multiply_fusion.3, f32[4096]{0:T(1024)S(1)} %fusion.77), kind=kLoop, calls=%fused_computation.40 | loop fusion | flops 25690112 | bytes 29392896 | tf_op jit(solution)/shard_map/transpose(jvp())/add_any | solution.py:14
  362.4 3.0 copy-done.3
  365.4 26.4 %convolution_convert_fusion.2 = bf16[2560,896]{1,0:T(8,128)(2,1)} fusion(bf16[4096,2560]{1,0:T(8,128)(2,1)} %get-tuple-element.30, bf16[4096,896]{0,1:T(8,128)(2,1)S(1)} %fusion.22), kind=kOutput, calls=%fused_computation.67 | convolution fusion | flops 18792775680 | bytes 32899072 | tf_op jit(solution)/shard_map/transpose(jvp())/dot_general | solution.py:10
  391.8 0.0 reduce-scatter.17.cloned.1.call-start
  391.8 36.2 %fusion.29 = bf16[2560,896]{1,0:T(8,128)(2,1)} fusion(bf16[1,4096,896]{2,1,0:T(8,128)(2,1)} %param.12, f32[4096,2560]{1,0:T(8,128)} %fusion.39, f32[4096,2560]{1,0:T(8,128)} %get-tuple-element.35), kind=kOutput, calls=%fused_computation.63 | convolution fusion | flops 18855690240 | bytes 95813632 | tf_op jit(solution)/shard_map/transpose(jvp())/dot_general | solution.py:10
  428.1 0.0 reduce-scatter.11.cloned.1.call-start
  428.1 27.7 %convolution_convert_fusion = bf16[4096,2560]{1,0:T(8,128)(2,1)} fusion(bf16[4096,896]{0,1:T(8,128)(2,1)} %copy-done.3, bf16[1,2560,896]{2,1,0:T(8,128)(2,1)} %all-gather.17.cloned.1.call-done), kind=kOutput, calls=%fused_computation.26 | convolution fusion | flops 18800967680 | bytes 32899072 | tf_op jit(solution)/shard_map/transpose(jvp())/dot_general | solution.py:10
  455.9 34.1 %fusion.36 = bf16[896,2560]{1,0:T(8,128)(2,1)} fusion(bf16[4096,2560]{1,0:T(8,128)(2,1)} %convolution_convert_fusion, f32[4096,2560]{1,0:T(8,128)} %fusion.47, bf16[1,4096,896]{1,2,0:T(8,128)(2,1)} %copy.20, f32[4096]{0:T(1024)S(1)} %copy-done.10), kind=kOutput, calls=%fused_computation.66 | convolution fusion | flops 18866700288 | bytes 74858496 | tf_op jit(solution)/shard_map/transpose(jvp())/dot_general | solution.py:22
  490.0 0.0 reduce-scatter.13.cloned.1.call-start
  490.1 34.2 %fusion.32 = bf16[896,2560]{1,0:T(8,128)(2,1)} fusion(bf16[4096,2560]{1,0:T(8,128)(2,1)} %convolution_convert_fusion.1, bf16[4096,896]{0,1:T(8,128)(2,1)} %get-tuple-element.33, f32[4096]{0:T(1024)S(1)} %copy-done.6, f32[4096,2560]{1,0:T(8,128)} %get-tuple-element.35), kind=kOutput, calls=%fused_computation.64 | convolution fusion | flops 18866700288 | bytes 74858496 | tf_op jit(solution)/shard_map/transpose(jvp())/dot_general | solution.py:22
  524.3 0.0 reduce-scatter.7.cloned.1.call-start
  524.3 42.0 %fusion.33 = bf16[896,2560]{1,0:T(8,128)(2,1)} fusion(f32[4096,2560]{1,0:T(8,128)} %fusion.47, f32[4096,2560]{1,0:T(8,128)} %get-tuple-element.31, bf16[4096,2560]{1,0:T(8,128)(2,1)} %convolution_convert_fusion, bf16[1,4096,896]{1,2,0:T(8,128)(2,1)} %copy.20, f32[4096]{0:T(1024)S(1)} %copy-done.10), kind=kOutput, calls=%fused_computation.65 | convolution fusion | flops 18919129088 | bytes 116801536 | tf_op jit(solution)/shard_map/transpose(jvp())/dot_general | solution.py:21
  566.4 0.0 reduce-scatter.9.cloned.1.call-start
  566.4 25.3 %convolution_convert_fusion.3 = bf16[896,2560]{1,0:T(8,128)(2,1)} fusion(bf16[4096,2560]{1,0:T(8,128)(2,1)} %get-tuple-element.34, bf16[4096,896]{0,1:T(8,128)(2,1)} %get-tuple-element.33, f32[4096]{0:T(1024)S(1)} %copy-done.6), kind=kOutput, calls=%fused_computation.68 | convolution fusion | flops 18801491968 | bytes 32915456 | tf_op jit(solution)/shard_map/transpose(jvp())/dot_general | solution.py:21
  591.7 0.0 all-reduce.3.cloned.1.call-start
  591.9 32.1 %reduce-scatter.7.cloned.1.call-done = bf16[224,2560]{1,0:T(8,128)(2,1)} async-done(((bf16[896,2560]{1,0:T(8,128)(2,1)}), bf16[224,2560]{1,0:T(8,128)(2,1)}) %reduce-scatter.7.cloned.1.call-update) | async-done | bytes 1146896 | tf_op jit(solution)/shard_map/reduce_scatter | solution.py:43
  624.0 45.6 %reduce-scatter.9.cloned.1.call-done = bf16[224,2560]{1,0:T(8,128)(2,1)} async-done(((bf16[896,2560]{1,0:T(8,128)(2,1)}), bf16[224,2560]{1,0:T(8,128)(2,1)}) %reduce-scatter.9.cloned.1.call-update) | async-done | bytes 1146896 | tf_op jit(solution)/shard_map/reduce_scatter | solution.py:43
  669.5 144.6 %all-reduce.3.cloned.1.call-done = (bf16[1,224,2560]{2,1,0:T(8,128)(2,1)}, bf16[1,224,2560]{2,1,0:T(8,128)(2,1)}, bf16[1,224,2560]{2,1,0:T(8,128)(2,1)}, bf16[1,...) async-done(((bf16[1,224,2560]{2,1,0:T(8,128)(2,1)}, bf16[1,224,2560]{2,1,0:T(8,128)(2,1)}, bf16[1,224,2560]{2,1,0:T(8,128)(2,1)}, ...) | async-done | bytes 6881296 | tf_op jit(solution)/shard_map/psum | solution.py:43
  814.2 3.4 fusion.57
  817.6 3.4 fusion.56
  820.9 3.4 fusion.55
  826.3 6.8 psum.55
  833.8 9.5 %fusion.63 = (bf16[2,640,896]{2,1,0:T(8,128)(2,1)}, f32[2,640,896]{2,1,0:T(8,128)}, f32[2,640,896]{2,1,0:T(8,128)}) fusion(bf16[2,640,896]{2,1,0:T(8,128)(2,1)} %param.15, f32[]{:T(128)S(6)} %min_shard_map.3, bf16[1,640,896]{2,1,0:T(8,128)(2,1)} %get-tuple-element.13, bf16[1,640,896]{2,1,0:T(8,128)(2,1)} %get-tuple-element.14, f32[2,640,896]{2,1,0:T(8,128)} %param.21, ...), kind=kLoop, calls=%fused_computation.87 | loop fusion | flops 22937600 | bytes 25231364 | tf_op jit(solution)/shard_map/convert_element_type | solution.py:30
  843.3 14.6 %fusion.54 = (bf16[2,224,2560]{2,1,0:T(8,128)(2,1)}, f32[2,224,2560]{2,1,0:T(8,128)}, f32[2,224,2560]{2,1,0:T(8,128)}, bf16[2,224,2560]{2,1,0:T(8,128)(2,1)}, f3...) fusion(bf16[2,224,2560]{2,1,0:T(8,128)(2,1)S(1)} %copy-done, f32[]{:T(128)S(6)} %min_shard_map.3, ...), kind=kLoop, calls=%fused_computation.78 | loop fusion | flops 45875200 | bytes 50462724 | tf_op jit(solution)/shard_map/convert_element_type | solution.py:30
  (46 shorter events, 0.5 us)
Async XLA Ops:
  7.2 6.6 copy-start.2
  7.2 41.0 %all-gather.13.cloned.1.call-start = ((), (), s32[]{:S(2)}) async-start(), calls=%async_computation.12 | async-start | bytes 5734400 | tf_op jit(solution)/shard_map/all_gather | solution.py:40
  10.5 74.5 %all-gather.15.cloned.1.call-start = ((), (), s32[]{:S(2)}) async-start(), calls=%async_computation.13 | async-start | bytes 5734400 | tf_op jit(solution)/shard_map/all_gather | solution.py:40
  13.8 121.0 %all-gather.17.cloned.1.call-start = ((), (), s32[]{:S(2)}) async-start(), calls=%async_computation.14 | async-start | bytes 5734400 | tf_op jit(solution)/shard_map/all_gather | solution.py:40
  15.4 146.8 %all-gather.23.cloned.1.call-start = ((), (), s32[]{:S(2)}) async-start(), calls=%async_computation.17 | async-start | bytes 5734400 | tf_op jit(solution)/shard_map/all_gather | solution.py:40
  16.0 179.3 %all-gather.21.cloned.1.call-start = ((), (), s32[]{:S(2)}) async-start(), calls=%async_computation.16 | async-start | bytes 5734400 | tf_op jit(solution)/shard_map/all_gather | solution.py:40
  16.6 215.3 %all-gather.19.cloned.1.call-start = ((), (), s32[]{:S(2)}) async-start(), calls=%async_computation.15 | async-start | bytes 5734400 | tf_op jit(solution)/shard_map/all_gather | solution.py:40
  17.1 574.7 %reduce-scatter.15.cloned.1.call-start = ((), (), s32[]{:S(2)}) async-start(), calls=%async_computation.10 | async-start | bytes 5734400 | tf_op jit(solution)/shard_map/reduce_scatter | solution.py:43
  32.5 52.5 %copy-start.9 = (f32[4096]{0:T(1024)}, f32[4096]{0:T(1024)S(1)}, u32[]{:S(2)}) copy-start(f32[4096]{0:T(1024)S(1)} %add_rsqrt_fusion) | copy-start | bytes 49156
  161.5 0.6 copy-start.7
  162.2 190.4 %copy-start.5 = (f32[4096]{0:T(1024)}, f32[4096]{0:T(1024)S(1)}, u32[]{:S(2)}) copy-start(f32[4096]{0:T(1024)S(1)} %fusion.77) | copy-start | bytes 49156
  231.9 58.3 %copy-start.11 = (bf16[1,896,2560]{2,1,0:T(8,128)(2,1)S(1)}, bf16[1,896,2560]{2,1,0:T(8,128)(2,1)}, u32[]{:S(2)}) copy-start(bf16[1,896,2560]{2,1,0:T(8,128)(2,1)} %all-gather.19.cloned.1.call-done) | copy-start | bytes 13762564
  313.8 38.7 %copy-start.8 = (f32[4096]{0:T(1024)S(1)}, f32[4096]{0:T(1024)}, u32[]{:S(2)}) copy-start(f32[4096]{0:T(1024)} %copy-done.7) | copy-start | bytes 49156
  362.4 3.0 copy-start.3
  391.8 200.0 %reduce-scatter.17.cloned.1.call-start = ((), (), s32[]{:S(2)}) async-start(), calls=%async_computation.11 | async-start | bytes 5734400 | tf_op jit(solution)/shard_map/reduce_scatter | solution.py:43
  428.1 27.8 %copy-start.10 = (f32[4096]{0:T(1024)S(1)}, f32[4096]{0:T(1024)}, u32[]{:S(2)}) copy-start(f32[4096]{0:T(1024)} %copy-done.9) | copy-start | bytes 49156
  428.1 163.8 %reduce-scatter.11.cloned.1.call-start = ((), (), s32[]{:S(2)}) async-start(), calls=%async_computation.8 | async-start | bytes 5734400 | tf_op jit(solution)/shard_map/reduce_scatter | solution.py:43
  455.9 34.2 %copy-start.6 = (f32[4096]{0:T(1024)S(1)}, f32[4096]{0:T(1024)}, u32[]{:S(2)}) copy-start(f32[4096]{0:T(1024)} %copy-done.5) | copy-start | bytes 49156
  490.0 101.9 %reduce-scatter.13.cloned.1.call-start = ((), (), s32[]{:S(2)}) async-start(), calls=%async_computation.9 | async-start | bytes 5734400 | tf_op jit(solution)/shard_map/reduce_scatter | solution.py:43
  524.3 99.7 %reduce-scatter.7.cloned.1.call-start = ((), (), s32[]{:S(2)}) async-start(), calls=%async_computation.6 | async-start | bytes 5734400 | tf_op jit(solution)/shard_map/reduce_scatter | solution.py:43
  566.4 103.2 %reduce-scatter.9.cloned.1.call-start = ((), (), s32[]{:S(2)}) async-start(), calls=%async_computation.7 | async-start | bytes 5734400 | tf_op jit(solution)/shard_map/reduce_scatter | solution.py:43
  591.7 222.4 %all-reduce.3.cloned.1.call-start = ((), (), s32[]{:S(2)}) async-start(), calls=%async_computation.18 | async-start | bytes 13762560 | tf_op jit(solution)/shard_map/psum | solution.py:43
  833.8 9.5 %copy-start = (bf16[2,224,2560]{2,1,0:T(8,128)(2,1)S(1)}, bf16[2,224,2560]{2,1,0:T(8,128)(2,1)}, u32[]{:S(2)}) copy-start(bf16[2,224,2560]{2,1,0:T(8,128)(2,1)} %param.13) | copy-start | bytes 6881284
  833.8 9.5 %copy-start.1 = (bf16[2,224,2560]{2,1,0:T(8,128)(2,1)S(1)}, bf16[2,224,2560]{2,1,0:T(8,128)(2,1)}, u32[]{:S(2)}) copy-start(bf16[2,224,2560]{2,1,0:T(8,128)(2,1)} %param.14) | copy-start | bytes 6881284
  833.8 9.5 %copy-start.4 = (bf16[1,224,2560]{2,1,0:T(8,128)(2,1)S(1)}, bf16[1,224,2560]{2,1,0:T(8,128)(2,1)}, u32[]{:S(2)}) copy-start(bf16[1,224,2560]{2,1,0:T(8,128)(2,1)} %get-tuple-element.9) | copy-start | bytes 3440644
Sparse Core Ops, SparseCore 0:
  10.7 37.4 all-gather.12
  50.3 34.6 all-gather.14
  87.2 34.6 all-gather.16
  123.8 34.6 all-gather.22
  160.5 34.6 all-gather.20
  197.2 34.6 all-gather.18
  391.9 42.5 reduce-scatter.14
  437.6 42.5 reduce-scatter.16
  490.1 42.5 reduce-scatter.10
  535.7 42.5 reduce-scatter.12
  581.4 42.5 reduce-scatter.6
  626.9 42.5 reduce-scatter.8
  674.1 140.0 all-reduce.2
where the time goes:
time: 872 us; the launch traced here: 865 us
  matrix products  511 us (59%)
  waiting for transfers between devices  248 us (28%)
  other arithmetic  48.6 us (6%)
  local copies, waits for them, and re-layouts  33.1 us (4%)
  between operations  17 us (2%)
    dot_general x5, matrix products, layer(): up = jnp.dot(a, w['w_up'], preferred_element_type=jnp.float32)  186 us
    dot_general x5, matrix products, layer(): gate = jnp.dot(a, w['w_gate'], preferred_element_type=jnp.float32)  179 us
    dot_general x5, matrix products, matmul(): jnp.dot(a, w, preferred_element_type=jnp.float32).astype(jnp.bfloat16)  146 us
    psum x1, waiting for transfers between devices, summed(): lax.psum(lax.psum_scatter(term, 's', scatter_dimension=0, tiled=True), 'r')  145 us
    reduce_scatter x6, waiting for transfers between devices, summed(): lax.psum_scatter(term, 's', scatter_dimension=0, tiled=True)  77.7 us
    unnamed x26, local copies, waits for them, and re-layouts  25.1 us
    all_gather x6, waiting for transfers between devices, fetched(): lax.all_gather(w[number], 's', axis=0, tiled=True)  24.1 us
    convert_element_type x2, other arithmetic, adamw(): return ((w - 0.02 * step).astype(jnp.bfloat16), m, v)  24.1 us
  transfers between devices with their start and end apart: 13, of which 7 were waited for; matrix products, arithmetic and copies ran while one was open for 46% of the time, Pallas kernels for 0%

commit v1 on v0

v1 whole, which is shorter than its diff:
```python
import functools

import jax
import jax.numpy as jnp
from jax import lax
from jax.experimental import pallas as pl
from jax.experimental.pallas import tpu as pltpu
from jax.sharding import PartitionSpec as P

NAMES = ("w_gate", "w_up", "w_down")
F32, BF16 = jnp.float32, jnp.bfloat16
MESH = pl.DeviceIdType.MESH
VMEM_LIMIT = 60 * 1024 * 1024
SMALL = VMEM_LIMIT


def dot(a, b, dims):
    return lax.dot_general(a, b, (dims, ((), ())), preferred_element_type=F32)


NN, NT, TN = ((1,), (0,)), ((1,), (1,)), ((0,), (0,))


def normed(h):
    wide = h.astype(F32)
    scale = lax.rsqrt(jnp.mean(wide * wide, -1, keepdims=True) + 1e-6)
    return (wide * scale).astype(BF16)


def call(body, name, grid, in_specs, out_specs, out_shape, scratch, flops, moved, sends=None, limit=VMEM_LIMIT):
    remote = {} if sends is None else {"collective_id": sends, "has_side_effects": True}
    return pl.pallas_call(
        body,
        grid=grid,
        in_specs=in_specs,
        out_specs=out_specs,
        out_shape=out_shape,
        scratch_shapes=scratch,
        name=name,
        compiler_params=pltpu.CompilerParams(dimension_semantics=("arbitrary",) * len(grid), vmem_limit_bytes=limit, **remote),
        cost_estimate=pl.CostEstimate(flops=flops, bytes_accessed=moved, transcendentals=0),
    )


def once(shape, index):
    return pl.BlockSpec(shape, index, pipeline_mode=pl.Buffered(1))


def shape(dims, dtype):
    return jax.ShapeDtypeStruct(dims, dtype)


class Place:
    def __init__(self):
        s, r = lax.axis_index("s"), lax.axis_index("r")
        self.s, self.r = s, r
        self.x, self.c = s // 2, s % 2
        self.s_core, self.s_x = s + 1 - 2 * self.c, (s + 2) % 4
        self.s_both = (self.s_core + 2) % 4
        self.r_y, self.r_z = (r + 2) % 4, r + 1 - 2 * (r % 2)
        self.r_yz = (self.r_z + 2) % 4
        self.core, self.over_x = {"s": self.s_core}, {"s": self.s_x}
        self.over_y, self.over_z = {"r": self.r_y}, {"r": self.r_z}

    def meet(self):
        barrier = pltpu.get_barrier_semaphore()
        for one in (self.core, self.over_x, self.over_y, self.over_z):
            pl.semaphore_signal(barrier, inc=1, device_id=one, device_id_type=MESH)
        pl.semaphore_wait(barrier, 4)


def remote(src, dst, send, recv, device):
    return pltpu.make_async_remote_copy(
        src_ref=src, dst_ref=dst, send_sem=send, recv_sem=recv, device_id=device, device_id_type=MESH
    )


class Sum:
    PHASES = 5

    def __init__(self, place, refs, out, square, scratch):
        self.place, self.refs, self.out, self.square = place, refs, out, square
        self.kept, self.got, self.far, self.got_x, self.near, self.got_1, self.pair, self.got_2, self.local, self.send, self.recv = scratch
        half = self.far.shape[0] // 2
        self.top, self.low = pl.ds(0, half), pl.ds(half, half)

    @staticmethod
    def scratch(rows, cols):
        one = lambda *lead: pltpu.VMEM((*lead, rows, cols), BF16)
        sems = [pltpu.SemaphoreType.DMA((k,)) for k in (2, 7, 7)]
        return [one(2), one(2), one(), one(), one(), one(), one(), one(), *sems]

    def copies(self, phase):
        p, over = self.place, lambda i, src, dst, to: remote(src, dst, self.send.at[i], self.recv.at[i], to)
        if phase == 0:
            return [over(i, self.refs[2 + i], self.got.at[i], p.core) for i in range(2)]
        if phase == 1:
            return [over(2, self.far, self.got_x, p.over_x)]
        if phase == 2:
            return [
                over(3, self.near.at[self.top], self.got_1.at[self.top], p.over_y),
                over(4, self.near.at[self.low], self.got_1.at[self.low], p.over_z),
            ]
        return [
            over(5, self.pair.at[self.top], self.got_2.at[self.top], p.over_z),
            over(6, self.pair.at[self.low], self.got_2.at[self.low], p.over_y),
        ]

    def locals(self):
        return [pltpu.make_async_copy(self.refs[i], self.kept.at[i], self.local.at[i]) for i in range(2)]

    def run(self, phase):
        x = self.place.x
        wide = lambda ref: ref.astype(F32)
        if phase == 0:
            for one in self.locals() + self.copies(0):
                one.start()
            return
        for one in self.copies(phase - 1):
            one.wait()
        if phase == 1:
            for one in self.locals():
                one.wait()
            self.far[...] = (wide(self.kept[1 - x]) + wide(self.got[1 - x])).astype(BF16)
        elif phase == 2:
            self.near[...] = (wide(self.kept[x]) + wide(self.got[x]) + wide(self.got_x[...])).astype(BF16)
        elif phase == 3:
            self.pair[...] = (wide(self.near[...]) + wide(self.got_1[...])).astype(BF16)
        else:
            total = (wide(self.pair[...]) + wide(self.got_2[...])).astype(BF16)
            self.out[...] = total
            self.square[...] = jnp.full(self.square.shape, jnp.sum(wide(total) * wide(total)), F32)
            return
        for one in self.copies(phase):
            one.start()


class Load:
    def __init__(self, terms, id):
        self.terms, self.id = terms, id
        self.sizes = [one[0].shape for one in terms]
        self.args = [ref for one in terms for ref in one]
        self.in_specs = [pl.BlockSpec(memory_space=pl.ANY)] * len(self.args)
        here = lambda *_: (0, 0)
        self.out_specs = [once(size, here) for one in self.sizes for size in (one, (8, 128))]
        self.out_shape = [shape(size, dtype) for one in self.sizes for size, dtype in ((one, BF16), ((8, 128), F32))]
        self.scratch = [ref for size in self.sizes for ref in Sum.scratch(*size)]

    def sums(self, place, ins, outs, scratch):
        per = len(scratch) // len(self.sizes)
        return [
            Sum(place, ins[4 * i : 4 * i + 4], outs[2 * i], outs[2 * i + 1], scratch[per * i : per * i + per])
            for i in range(len(self.sizes))
        ]

    def drive(self, place, sums, step, at):
        for phase, when in enumerate(at):

            @pl.when(step == when)
            def _(phase=phase):
                if phase == 0:
                    place.meet()
                for one in sums:
                    one.run(phase)

    def results(self, outs):
        return list(zip(outs[0::2], outs[1::2]))


def carried(body, load, own_in, own_out, at):
    if load is None:
        return body

    def both(*refs):
        n_in, n_out, n_scratch = len(load.in_specs), len(load.out_specs), len(load.scratch)
        ins, refs = refs[:own_in], refs[own_in:]
        more_in, refs = refs[:n_in], refs[n_in:]
        outs, refs = refs[:own_out], refs[own_out:]
        more_out, refs = refs[:n_out], refs[n_out:]
        scratch, more_scratch = refs[: len(refs) - n_scratch], refs[len(refs) - n_scratch :]
        place = Place()
        load.drive(place, load.sums(place, more_in, more_out, more_scratch), pl.program_id(0), at)
        body(*ins, *outs, *scratch)

    return both


def call_with(load, at, body, name, grid, in_specs, out_specs, out_shape, scratch, flops, moved, args):
    if load is None:
        outs = call(body, name, grid, in_specs, out_specs, out_shape, scratch, flops, moved)(*args)
        return list(outs), []
    outs = call(
        carried(body, load, len(in_specs), len(out_specs), at),
        name,
        grid,
        in_specs + load.in_specs,
        out_specs + load.out_specs,
        out_shape + load.out_shape,
        scratch + load.scratch,
        flops,
        moved,
        load.id,
    )(*args, *load.args)
    return list(outs[: len(out_specs)]), load.results(outs[len(out_specs) :])


def spread(acc, rows, refs):
    c = lax.axis_index("s") % 2
    for i, ref in enumerate(refs):
        at = (i % 2) * 2 + (c if i < 2 else 1 - c)
        ref[...] = acc[pl.ds(pl.multiple_of(at * rows, rows), rows), :].astype(BF16)


def spread_shapes(rows, cols, count=4):
    return [shape((rows, cols), BF16)] * count


def spread_specs(rows, cols, count=4):
    return [once((rows, cols), lambda *_: (0, 0))] * count


def clear(step, *refs):
    @pl.when(step == 0)
    def _():
        for ref in refs:
            ref[...] = jnp.zeros_like(ref)


class Fetch:
    COPIES = 9

    def __init__(self, place, own, full, columns, send, recv, local, stage=None):
        self.place, self.own, self.full, self.columns = place, own, full, columns
        self.send, self.recv, self.local, self.stage = send, recv, local, stage

    def part(self, block, quarter=None):
        rows = self.own.shape[0]
        if self.columns is None:
            if quarter is None:
                return self.full.at[pl.ds(pl.multiple_of(block * rows, rows), rows)]
            return self.full.at[pl.ds(pl.multiple_of(block * rows + quarter * (rows // 4), rows // 4), rows // 4)]
        start, width = self.columns
        across = pl.ds(start, width) if quarter is None else pl.ds(pl.multiple_of(start + quarter * (width // 4), 128), width // 4)
        return self.full.at[pl.ds(pl.multiple_of(block * rows, rows), rows), across]

    def mine(self, quarter=None):
        rows = self.own.shape[0]
        if self.columns is None:
            return self.own if quarter is None else self.own.at[pl.ds(pl.multiple_of(quarter * (rows // 4), rows // 4), rows // 4)]
        start, width = self.columns
        across = pl.ds(start, width) if quarter is None else pl.ds(pl.multiple_of(start + quarter * (width // 4), 128), width // 4)
        return self.own.at[:, across]

    def copy(self, i):
        p = self.place
        over = lambda src, dst, to: remote(src, dst, self.send.at[i], self.recv.at[i], to)
        if i == 0:
            return over(self.mine(), self.part(p.s), p.core)
        if i in (1, 2):
            q = p.r if i == 1 else p.r_yz
            return over(self.mine(q), self.part(p.s, q), p.over_x)
        if i in (3, 4):
            return over(self.part(p.s_x, p.r), self.part(p.s_x, p.r), p.over_y if i == 3 else p.over_z)
        q = (p.r, p.r_yz, p.r_y, p.r_z)[i - 5]
        return over(self.part(p.s_x, q), self.part(p.s_x, q), p.core)

    def start(self, *which):
        for i in which:
            self.copy(i).start()

    def arrived(self, i):
        self.copy(i).wait_recv()

    def begin(self):
        self.start(1, 2, 0)
        into = self.stage if self.stage is not None else self.part(self.place.s)
        pltpu.make_async_copy(self.mine(), into, self.local.at[0]).start()

    def relay(self):
        self.arrived(1)
        self.start(3, 4, 5)
        if self.stage is not None:
            pltpu.make_async_copy(self.mine(), self.stage, self.local.at[0]).wait()
            pltpu.make_async_copy(self.stage, self.part(self.place.s), self.local.at[1]).start()

    def hand_over(self):
        self.arrived(2)
        self.start(6)
        self.arrived(3)
        self.start(7)
        self.arrived(4)
        self.start(8)

    def finish(self):
        if self.stage is not None:
            pltpu.make_async_copy(self.stage, self.part(self.place.s), self.local.at[1]).wait()
        else:
            pltpu.make_async_copy(self.mine(), self.part(self.place.s), self.local.at[0]).wait()
        for i in (0, 5, 6, 7, 8):
            self.arrived(i)
        for i in range(self.COPIES):
            self.copy(i).wait_send()


RUN, HEAD = 512, 1024


def project_body(h_ref, *refs):
    own, refs = [ref.at[number] for number in range(2) for ref in refs[:3]], refs[3:]
    gate_ref, up_ref, prod_ref = refs[:3]
    full, refs = refs[3:7], refs[7:]
    a_all, wg, wu, stage_d0, stage_g1, stage_u1, stage_d1, send, recv, local = refs
    run, tile = pl.program_id(0), pl.program_id(1)
    step = run * pl.num_programs(1) + tile
    place = Place()
    ff = wg.shape[1]
    plan = [
        (own[0], wg, (0, HEAD), None),
        (own[1], wu, (0, HEAD), None),
        (own[0], wg, (HEAD, ff - HEAD), None),
        (own[1], wu, (HEAD, ff - HEAD), None),
        (own[2], full[0], None, stage_d0),
        (own[3], full[1], (0, ff), stage_g1),
        (own[4], full[2], (0, ff), stage_u1),
        (own[5], full[3], None, stage_d1),
    ]
    fetches = [
        Fetch(place, mine, whole, columns, send.at[i], recv.at[i], local.at[i], stage) for i, (mine, whole, columns, stage) in enumerate(plan)
    ]

    @pl.when(step == 0)
    def _():
        place.meet()
        a, b, c, d = fetches[:4]
        for one in (a, b):
            one.begin()
        for one in (c, d):
            one.begin()
        for one in (a, b):
            one.relay()
        for one in (a, b):
            one.hand_over()
        for one in (a, b):
            one.finish()

    for when, number, what in (
        (1, 2, "relay"),
        (1, 3, "relay"),
        (1, 4, "begin"),
        (3, 2, "hand_over"),
        (3, 3, "hand_over"),
        (4, 4, "relay"),
        (4, 5, "begin"),
        (5, 4, "hand_over"),
        (7, 2, "finish"),
        (7, 3, "finish"),
        (8, 5, "relay"),
        (8, 6, "begin"),
        (10, 4, "finish"),
        (11, 5, "hand_over"),
        (11, 6, "relay"),
        (11, 7, "begin"),
        (14, 6, "hand_over"),
        (14, 7, "relay"),
        (17, 7, "hand_over"),
        (18, 5, "finish"),
        (18, 6, "finish"),
        (19, 7, "finish"),
    ):

        @pl.when(step == when)
        def _(number=number, what=what):
            getattr(fetches[number], what)()

    rows = h_ref.shape[0]
    mine = pl.ds(pl.multiple_of(tile * rows, rows), rows)

    @pl.when(run == 0)
    def _():
        a_all[mine, :] = normed(h_ref[...])

    a = a_all[mine, :]
    across = pl.ds(pl.multiple_of(run * RUN, RUN), RUN)
    gate = dot(a, wg[:, across], NN)
    up = dot(a, wu[:, across], NN)
    gate_ref[...] = gate
    up_ref[...] = up
    prod_ref[...] = (gate * jax.nn.sigmoid(gate) * up).astype(BF16)


def project(h, weights, tile=1024):
    n, d = h.shape
    ff = weights[0].shape[2]
    sizes = [one.shape[1:] for one in (weights[2], *weights)]
    rows = pl.BlockSpec((tile, RUN), lambda i, j: (j, i))
    hbm = pl.BlockSpec(memory_space=pl.ANY)
    outs = call(
        project_body,
        "project",
        (ff // RUN, n // tile),
        [pl.BlockSpec((tile, d), lambda i, j: (jnp.where(i == 0, j, n // tile - 1), 0))] + [hbm] * 3,
        [rows] * 3 + [hbm] * 4,
        [shape((n, ff), F32), shape((n, ff), F32), shape((n, ff), BF16)]
        + [shape((rows_ * 4, cols), BF16) for rows_, cols in sizes],
        [pltpu.VMEM((n, d), BF16), pltpu.VMEM((d, ff), BF16), pltpu.VMEM((d, ff), BF16)]
        + [pltpu.VMEM(size, BF16) for size in sizes]
        + [pltpu.SemaphoreType.DMA((8, 9)), pltpu.SemaphoreType.DMA((8, 9)), pltpu.SemaphoreType.DMA((8, 2))],
        4 * n * d * ff,
        n * ff * 10,
        0,
    )(h, *weights)
    return outs[:3], outs[3:]


def down_body(h_ref, prod_ref, wd_ref, out_ref):
    out_ref[...] = h_ref[...] + dot(prod_ref[...], wd_ref[...], NN).astype(BF16)


def down(h, prod, wd, tile=512):
    n, d = h.shape
    ff = wd.shape[0]
    rows = lambda width: pl.BlockSpec((tile, width), lambda i: (i, 0))
    return call(
        down_body,
        "down",
        (n // tile,),
        [rows(d), rows(ff), once((ff, d), lambda i: (0, 0))],
        rows(d),
        shape((n, d), BF16),
        [],
        2 * n * d * ff,
        n * ff * 2,
    )(h, prod, wd)


def slopes(gate, up, dprod):
    s = jax.nn.sigmoid(gate)
    silu = gate * s
    return silu, (dprod * silu).astype(BF16), (dprod * up * (s + silu * (1 - s))).astype(BF16)


def last_body(part, h_ref, dy_ref, wg_ref, wu_ref, wd_ref, dgate_ref, dup_ref, *rest):
    outs, (acc_g, acc_u, acc_d) = rest[:10], rest[10:]
    step = pl.program_id(0)
    clear(step, acc_g, acc_u, acc_d)
    a = normed(h_ref[...])
    dy = dy_ref[...]
    a_t, dy_t = a.T, dy.T
    parts = [slice(i, i + part) for i in range(0, wg_ref.shape[1], part)]
    front = lambda at: (dot(a, wg_ref[:, at], NN), dot(a, wu_ref[:, at], NN), dot(dy, wd_ref[at, :], NT))
    ahead = front(parts[0])
    for i, at in enumerate(parts):
        gate, up, dprod = ahead
        if i + 1 < len(parts):
            ahead = front(parts[i + 1])
        silu, dup, dgate = slopes(gate, up, dprod.astype(BF16).astype(F32))
        dgate_ref[:, at] = dgate
        dup_ref[:, at] = dup
        acc_g[:, at] += dot(a_t, dgate, NN)
        acc_u[:, at] += dot(a_t, dup, NN)
        acc_d[:, at] += dot(dy_t, (silu * up).astype(BF16), NN)

    @pl.when(step == pl.num_programs(0) - 1)
    def _():
        rows = acc_g.shape[0] // 4
        spread(acc_g, rows, outs[:4])
        spread(acc_u, rows, outs[4:8])
        c = lax.axis_index("s") % 2
        rows = acc_d.shape[1] // 2
        for core, ref in ((c, outs[8]), (1 - c, outs[9])):
            ref[...] = acc_d[:, pl.ds(pl.multiple_of(core * rows, rows), rows)].T.astype(BF16)


def last(h, dy, wg, wu, wd, run, runs, load=None, at=(), tile=256, part=256):
    n, d = h.shape
    ff = wg.shape[1] // runs
    rows = lambda width: pl.BlockSpec((tile, width), lambda i: (i, 0))
    columns = lambda: once((d, ff), lambda i: (0, run))
    outs, done = call_with(
        load,
        at,
        functools.partial(last_body, part),
        f"last{run}",
        (n // tile,),
        [rows(d), rows(d), columns(), columns(), once((ff, d), lambda i: (run, 0))],
        [rows(ff), rows(ff)] + spread_specs(d // 4, ff, 8) + spread_specs(ff // 2, d, 2),
        [shape((n, ff), BF16)] * 2 + spread_shapes(d // 4, ff, 8) + spread_shapes(ff // 2, d, 2),
        [pltpu.VMEM((d, ff), F32)] * 3,
        12 * n * d * ff,
        n * ff * 4,
        (h, dy, wg, wu, wd),
    )
    return outs[0], outs[1], outs[2:6], outs[6:10], outs[10:12], done


def inward_body(runs, h_ref, by_ref, *rest):
    dgates, dups, (wg_ref, wu_ref, out_ref) = rest[:runs], rest[runs : 2 * runs], rest[2 * runs :]
    ff = dgates[0].shape[1]
    total = lambda parts, w: sum(dot(p[...], w[:, i * ff : (i + 1) * ff], NT) for i, p in enumerate(parts)).astype(BF16)
    da = (total(dgates, wg_ref) + total(dups, wu_ref)).astype(F32)
    wide = h_ref[...].astype(F32)
    scale = lax.rsqrt(jnp.mean(wide * wide, -1, keepdims=True) + 1e-6)
    along = jnp.mean(da * wide, -1, keepdims=True)
    dh = da * scale - wide * (scale * scale * scale * along)
    out_ref[...] = by_ref[...] + dh.astype(BF16)


def inward(h, by, dgates, dups, wg, wu, load=None, at=(), tile=512):
    n, d = h.shape
    ff = wg.shape[1]
    runs = len(dgates)
    rows = lambda width: pl.BlockSpec((tile, width), lambda i: (i, 0))
    outs, done = call_with(
        load,
        at,
        functools.partial(inward_body, runs),
        "inward",
        (n // tile,),
        [rows(d), rows(d)] + [rows(ff // runs)] * (2 * runs) + [once((d, ff), lambda i: (0, 0))] * 2,
        [rows(d)],
        [shape((n, d), BF16)],
        [],
        4 * n * d * ff,
        n * ff * 4,
        (h, by, *dgates, *dups, wg, wu),
    )
    return outs[0], done


def outer_body(by_ref, prod_ref, *rest):
    outs, acc = rest[:4], rest[4]
    step = pl.program_id(0)
    clear(step, acc)
    acc[...] += dot(by_ref[...].T, prod_ref[...], NN)

    @pl.when(step == pl.num_programs(0) - 1)
    def _():
        c = lax.axis_index("s") % 2
        rows = acc.shape[1] // 4
        for i, ref in enumerate(outs):
            block = (i % 2) * 2 + (c if i < 2 else 1 - c)
            ref[...] = acc[:, pl.ds(pl.multiple_of(block * rows, rows), rows)].T.astype(BF16)


def outer(by, prod, load=None, at=(), tile=512):
    n, d = by.shape
    ff = prod.shape[1]
    rows = lambda width: pl.BlockSpec((tile, width), lambda i: (i, 0))
    return call_with(
        load,
        at,
        outer_body,
        "outer",
        (n // tile,),
        [rows(d), rows(ff)],
        spread_specs(ff // 4, d),
        spread_shapes(ff // 4, d),
        [pltpu.VMEM((d, ff), F32)],
        2 * n * d * ff,
        n * ff * 2,
        (by, prod),
    )


def first_body(part, h_ref, by_ref, gate_ref, up_ref, wd_ref, *rest):
    outs, (acc_g, acc_u) = rest[:8], rest[8:]
    step = pl.program_id(0)
    clear(step, acc_g, acc_u)
    a_t = normed(h_ref[...]).T
    by = by_ref[...]
    parts = [slice(i, i + part) for i in range(0, wd_ref.shape[0], part)]
    front = lambda at: dot(by, wd_ref[at, :], NT)
    ahead = front(parts[0])
    for i, at in enumerate(parts):
        dprod = ahead.astype(BF16).astype(F32)
        if i + 1 < len(parts):
            ahead = front(parts[i + 1])
        _, dup, dgate = slopes(gate_ref[:, at], up_ref[:, at], dprod)
        acc_g[:, at] += dot(a_t, dgate, NN)
        acc_u[:, at] += dot(a_t, dup, NN)

    @pl.when(step == pl.num_programs(0) - 1)
    def _():
        rows = acc_g.shape[0] // 4
        spread(acc_g, rows, outs[:4])
        spread(acc_u, rows, outs[4:])


def first(h, by, gate, up, wd, run, width, load=None, at=(), tile=512, part=256):
    n, d = h.shape
    rows = lambda: pl.BlockSpec((tile, d), lambda i: (i, 0))
    kept = lambda: pl.BlockSpec((tile, width), lambda i: (i, run))
    outs, done = call_with(
        load,
        at,
        functools.partial(first_body, part),
        f"first{run}",
        (n // tile,),
        [rows(), rows(), kept(), kept(), once((width, d), lambda i: (run, 0))],
        spread_specs(d // 4, width, 8),
        spread_shapes(d // 4, width, 8),
        [pltpu.VMEM((d, width), F32)] * 2,
        6 * n * d * width,
        n * width * 8,
        (h, by, gate, up, wd),
    )
    return outs[:4], outs[4:], done


def tail_body(count, squares, load, *refs):
    n_in, n_out = len(load.in_specs), len(load.out_specs)
    others, refs = refs[:squares], refs[squares:]
    ins, refs = refs[:n_in], refs[n_in:]
    outs, factor_ref, refs = refs[:n_out], refs[n_out], refs[n_out + 1 :]
    scratch, (mine, got_core, both, got_x, send, recv) = refs[: len(load.scratch)], refs[len(load.scratch) :]
    place = Place()
    sums = load.sums(place, ins, outs, scratch)
    place.meet()
    for wave in range(len(sums) + Sum.PHASES - 1):
        for i, one in enumerate(sums):
            if i == 0 and wave == 0:
                for each in sums:
                    each.run(0)
            if 1 <= wave - i + 1 < Sum.PHASES:
                one.run(wave - i + 1)
    total = sum(ref[...] for ref in others) + sum(one.square[...] for one in sums)
    mine[...] = total
    hop = remote(mine, got_core, send.at[0], recv.at[0], place.core)
    hop.start()
    hop.wait()
    both[...] = mine[...] + got_core[...]
    hop = remote(both, got_x, send.at[1], recv.at[1], place.over_x)
    hop.start()
    hop.wait()
    factor_ref[...] = jnp.minimum(1.0, 0.5 * lax.rsqrt((both[...] + got_x[...]) / count + 1e-30))


def tail(load, squares, count):
    whole = pl.BlockSpec((8, 128), lambda: (0, 0))
    outs = call(
        functools.partial(tail_body, count, len(squares), load),
        "tail",
        (),
        [whole] * len(squares) + load.in_specs,
        [pl.BlockSpec(one.block_shape, lambda: (0, 0)) for one in load.out_specs] + [whole],
        load.out_shape + [shape((8, 128), F32)],
        load.scratch + [pltpu.VMEM((8, 128), F32)] * 4 + [pltpu.SemaphoreType.DMA((2,))] * 2,
        1000,
        1000,
        load.id,
        SMALL,
    )(*squares, *load.args)
    return load.results(outs[:-1]), outs[-1]


def adamw(w, m, v, g):
    m = 0.9 * m + 0.1 * g
    v = 0.95 * v + 0.05 * g * g
    step = m * lax.rsqrt(v + 1e-8) + 0.1 * w
    return (w - 0.02 * step).astype(BF16), m, v


def update_body(edges, factor_ref, *refs):
    counts = [[len(e) - 1 for e in one] for one in edges]
    total = sum(map(sum, counts))
    grads, refs = refs[:total], refs[total:]
    states, news = refs[:9], refs[9:]
    layer, turn = pl.program_id(0), pl.program_id(1)
    factor = factor_ref[0, 0]
    k = 0
    for i, per_layer in enumerate(edges):
        for number, edge in enumerate(per_layer):
            for low, high in zip(edge, edge[1:]):

                @pl.when((layer == number) & (turn >= low) & (turn < high))
                def _(ref=grads[k], i=i):
                    w, m, v = (states[3 * which + i][0] for which in range(3))
                    for which, one in enumerate(adamw(w.astype(F32), m, v, ref[...].astype(F32) * factor)):
                        news[3 * which + i][0] = one

                k += 1


def update(factor, pieces, states, turns=10):
    specs, edges, args = [pl.BlockSpec(memory_space=pltpu.SMEM)], [], [factor]
    state_specs = []
    for i, per_layer in enumerate(pieces):
        _, rows, cols = states[i].shape
        tall = i == 2
        block = (rows // turns, cols) if tall else (rows, cols // turns)
        edges.append([])
        for number, parts in enumerate(per_layer):
            edge = [0]
            for part in parts:
                low = edge[-1]
                edge.append(low + (part.shape[0] // block[0] if tall else part.shape[1] // block[1]))

                def index(layer, turn, number=number, low=low, top=edge[-1] - low - 1, tall=tall):
                    at = jnp.where(layer == number, jnp.clip(turn - low, 0, top), jnp.where(layer < number, 0, top))
                    return (at, 0) if tall else (0, at)

                specs.append(pl.BlockSpec(block, index))
                args.append(part)
            edges[-1].append(edge)
        state_specs.append(pl.BlockSpec((1, *block), (lambda layer, turn: (layer, turn, 0)) if tall else (lambda layer, turn: (layer, 0, turn))))
    return call(
        functools.partial(update_body, edges),
        "update",
        (2, turns),
        specs + state_specs * 3,
        state_specs * 3,
        [shape(one.shape, one.dtype) for one in states],
        [],
        1000000,
        1000000,
        limit=SMALL,
    )(*args, *states)


def solution(mesh):
    ns = mesh.shape["s"]

    def step(x, dy, *arrays):
        weights, m, v = (arrays[i : i + 3] for i in (0, 3, 6))
        h0, dy = x[0], dy[0]
        (gate, up, prod), (wd0, wg1, wu1, wd1) = project(h0, weights)
        h1 = down(h0, prod, wd0)
        a = last(h1, dy, wg1, wu1, wd1, 0, 2)
        b = last(h1, dy, wg1, wu1, wd1, 1, 2, Load([a[2], a[3]], 1), (0, 2, 6, 9, 12))
        (g1a, u1a) = b[5]
        by, (g1b, u1b) = inward(h1, dy, [a[0], b[0]], [a[1], b[1]], wg1, wu1, Load([b[2], b[3]], 2), (0, 1, 5, 6, 7))
        d0, (d1,) = outer(by, prod, Load([[a[4][0], b[4][0], a[4][1], b[4][1]]], 3), (0, 1, 5, 6, 7))
        c = first(h0, by, gate, up, wd0, 0, 1280, Load([d0], 4), (0, 1, 5, 6, 7))
        (d0,) = c[2]
        e = first(h0, by, gate, up, wd0, 1, 1280, Load([c[0], c[1]], 5), (0, 1, 5, 6, 7))
        g0a, u0a = e[2]
        done = [g1a, u1a, g1b, u1b, d1, d0, g0a, u0a]
        count = ns * sum(w.size for w in weights)
        (g0b, u0b), factor = tail(Load([e[0], e[1]], 6), [one[1] for one in done], count)
        parts = lambda *ones: [one[0] for one in ones]
        pieces = [
            [parts(g0a, g0b), parts(g1a, g1b)],
            [parts(u0a, u0b), parts(u1a, u1b)],
            [parts(d0), parts(d1)],
        ]
        return tuple(update(factor, pieces, [*weights, *m, *v]))

    states, cut = P(("rep", "r", "s"), None, None), P(None, "s", None)
    return jax.shard_map(
        step,
        mesh=mesh,
        in_specs=(states, states) + (cut,) * 9,
        out_specs=(P("rep", "s", None),) * 9,
        check_vma=False,
    )
```

time: 872 us -> 666 us (0.76)
  Pallas kernels: 0 us -> 657 us
  matrix products: 511 us -> 0 us
  waiting for transfers between devices: 248 us -> 0 us
  other arithmetic: 48.6 us -> 0 us
  local copies, waits for them, and re-layouts: 33.1 us -> 0 us
  between operations: 17 us -> 1.16 us
    pallas_call x0 -> x10, Pallas kernels: none -> 657 us  [the longest x5 371 us: call_with(): call(carried(body, load, len(in_specs), len(out_specs), at), name, grid,...]
    dot_general x15 -> x0, matrix products: 511 us -> none  [the longest x5 186 us: layer(): up = jnp.dot(a, w['w_up'], preferred_element_type=jnp.float32)]
    psum x1 -> x0, waiting for transfers between devices: 145 us -> none  [summed(): lax.psum(lax.psum_scatter(term, 's', scatter_dimension=0, tiled=True), 'r')]
    reduce_scatter x6 -> x0, waiting for transfers between devices: 77.7 us -> none  [summed(): lax.psum_scatter(term, 's', scatter_dimension=0, tiled=True)]
    unnamed x26 -> x0, local copies, waits for them, and re-layouts: 25.1 us -> none
    all_gather x6 -> x0, waiting for transfers between devices: 24.1 us -> none  [fetched(): lax.all_gather(w[number], 's', axis=0, tiled=True)]
    convert_element_type x2 -> x0, other arithmetic: 24.1 us -> none  [adamw(): return ((w - 0.02 * step).astype(jnp.bfloat16), m, v)]
    reduce_sum x4 -> x0, other arithmetic: 14.7 us -> none  [the longest x3 10.2 us: step(): squares = lax.psum(sum((jnp.sum(g * g) for g in gradients)), 's')]
  transfers between devices with their start and end apart: 13 -> 0, of which waited for: 7 -> 0; matrix products, arithmetic and copies ran while one was open for 46% -> 0% of each run, Pallas kernels for 0% -> 0%
where the time goes in v1:
time: 666 us; the launch traced here: 658 us
  Pallas kernels  657 us (99%)
    pallas_call x5, Pallas kernels, call_with(): call(carried(body, load, len(in_specs), len(out_specs), at), name, grid,...  371 us
    pallas_call x1, Pallas kernels, project(): call(project_body, 'project', (ff // RUN, n // tile), [pl.BlockSpec((tile...  94.2 us
    pallas_call x1, Pallas kernels, call_with(): call(body, name, grid, in_specs, out_specs, out_shape, scratch, flops, mo...  77 us
    pallas_call x1, Pallas kernels, tail(): call(functools.partial(tail_body, count, len(squares), load), 'tail', (),...  52.9 us
    pallas_call x1, Pallas kernels, update(): call(functools.partial(update_body, edges), 'update', (2, turns), specs +...  34 us
    pallas_call x1, Pallas kernels, down(): call(down_body, 'down', (n // tile,), [rows(d), rows(ff), once((ff, d), l...  27.7 us

profile of v1, /device:TPU:0, one launch (start us, length us, event | category | flops | bytes accessed | tf_op | source)
XLA Modules:
  0.0 658.1 jit_solution(2172564280604931995)
XLA Ops:
  0.6 94.2 %project.1 = (f32[4096,2560]{1,0:T(8,128)}, f32[4096,2560]{1,0:T(8,128)}, bf16[4096,2560]{1,0:T(8,128)(2,1)}, bf16[2560,896]{1,0:T(8,128)(2,1)}, bf16[896,2560]{...) custom-call(bf16[4096,896]{1,0:T(8,128)(2,1)} %bitcast.2, bf16[2,224,2560]{2,1,0:T(8,128)(2,1)} %refs_10_.1, ...), custom_call_target="tpu_custom_call" | custom-call | flops 37580963840 | bytes 104857600 | tf_op jit(solution)/shard_map/project/pallas_call | solution.py:397
  94.9 27.7 %down.1.h_ref.refs_0_ = bf16[4096,896]{1,0:T(8,128)(2,1)} custom-call(bf16[4096,896]{1,0:T(8,128)(2,1)} %bitcast.3, bf16[4096,2560]{1,0:T(8,128)(2,1)} %get-tuple-element.80.prod_ref.refs_1_, bf16[2560,896]{1,0:T(8,128)(2,1)} %get-tuple-element.81.wd_ref.refs_4_), custom_call_target="tpu_custom_call" | custom-call | flops 18790481920 | bytes 20971520 | tf_op jit(solution)/shard_map/down/pallas_call | solution.py:423
  122.6 77.0 %last0.1 = (bf16[4096,1280]{1,0:T(8,128)(2,1)}, bf16[4096,1280]{1,0:T(8,128)(2,1)}, bf16[224,1280]{1,0:T(8,128)(2,1)}, bf16[224,1280]{1,0:T(8,128)(2,1)}, bf16[2...) custom-call(bf16[4096,896]{1,0:T(8,128)(2,1)} %down.1.h_ref.refs_0_,, ...), custom_call_target="tpu_custom_call" | custom-call | flops 56371445760 | bytes 20971520 | tf_op jit(solution)/shard_map/last0/pallas_call | solution.py:190
  199.6 90.2 %last1.1 = (bf16[4096,1280]{1,0:T(8,128)(2,1)}, bf16[4096,1280]{1,0:T(8,128)(2,1)}, bf16[224,1280]{1,0:T(8,128)(2,1)}, bf16[224,1280]{1,0:T(8,128)(2,1)}, bf16[2...) custom-call(bf16[4096,896]{1,0:T(8,128)(2,1)} %down.1.h_ref.refs_0_,, ...), custom_call_target="tpu_custom_call" | custom-call | flops 56371445760 | bytes 20971520 | tf_op jit(solution)/shard_map/last1/pallas_call | solution.py:192
  289.9 72.8 %inward.1 = (bf16[4096,896]{1,0:T(8,128)(2,1)}, bf16[224,1280]{1,0:T(8,128)(2,1)}, f32[8,128]{1,0:T(8,128)}, bf16[224,1280]{1,0:T(8,128)(2,1)}, f32[8,128]{1,0:T(8,128)}) custom-call(bf16[4096,896]{1,0:T(8,128)(2,1)} %down.1.h_ref.refs_0_, bf16[4096,896]{1,0:T(8,128)(2,1)} %bitcast.8, bf16[4096,1280]{1,0:T(8,128)(2,1)} %get-tuple-element.95.refs_2_, ...), custom_call_target="tpu_custom_call" | custom-call | flops 37580963840 | bytes 41943040 | tf_op jit(solution)/shard_map/inward/pallas_call | solution.py:192
  362.7 70.0 %outer.1 = (bf16[640,896]{1,0:T(8,128)(2,1)}, bf16[640,896]{1,0:T(8,128)(2,1)}, bf16[640,896]{1,0:T(8,128)(2,1)}, bf16[640,896]{1,0:T(8,128)(2,1)}, bf16[640,896]{1,0:T(8,128)(2,1)}, /*index=5*/f32[8,128]{1,0:T(8,128)}) custom-call(bf16[4096,896]{1,0:T(8,128)(2,1)} %get-tuple-element.109.refs_0_.refs_1_, ...), custom_call_target="tpu_custom_call" | custom-call | flops 18790481920 | bytes 20971520 | tf_op jit(solution)/shard_map/outer/pallas_call | solution.py:192
  432.7 72.9 %first0.1 = (bf16[224,1280]{1,0:T(8,128)(2,1)}, bf16[224,1280]{1,0:T(8,128)(2,1)}, bf16[224,1280]{1,0:T(8,128)(2,1)}, bf16[224,1280]{1,0:T(8,128)(2,1)}, bf16[22...) custom-call(bf16[4096,896]{1,0:T(8,128)(2,1)} %bitcast.4, ...), custom_call_target="tpu_custom_call" | custom-call | flops 28185722880 | bytes 41943040 | tf_op jit(solution)/shard_map/first0/pallas_call | solution.py:192
  505.7 65.0 %first1.1 = (bf16[224,1280]{1,0:T(8,128)(2,1)}, bf16[224,1280]{1,0:T(8,128)(2,1)}, bf16[224,1280]{1,0:T(8,128)(2,1)}, bf16[224,1280]{1,0:T(8,128)(2,1)}, bf16[22...) custom-call(bf16[4096,896]{1,0:T(8,128)(2,1)} %bitcast.5, ...), custom_call_target="tpu_custom_call" | custom-call | flops 28185722880 | bytes 41943040 | tf_op jit(solution)/shard_map/first1/pallas_call | solution.py:192
  570.7 52.9 %tail.1 = (bf16[224,1280]{1,0:T(8,128)(2,1)}, f32[8,128]{1,0:T(8,128)}, bf16[224,1280]{1,0:T(8,128)(2,1)}, f32[8,128]{1,0:T(8,128)}, f32[8,128]{1,0:T(8,128)}) custom-call(f32[8,128]{1,0:T(8,128)} %get-tuple-element.93.refs_0_, f32[8,128]{1,0:T(8,128)} %get-tuple-element.94.refs_1_, f32[8,128]{1,0:T(8,128)} %get-tuple-element.107.refs_2_, ...), custom_call_target="tpu_custom_call" | custom-call | flops 1000 | bytes 1000 | tf_op jit(solution)/shard_map/tail/pallas_call | solution.py:640
  623.6 34.0 %update.1 = (bf16[2,224,2560]{2,1,0:T(8,128)(2,1)}, bf16[2,224,2560]{2,1,0:T(8,128)(2,1)}, bf16[2,640,896]{2,1,0:T(8,128)(2,1)}, f32[2,224,2560]{2,1,0:T(8,128)}...) custom-call(f32[8,128]{1,0:T(8,128)} %get-tuple-element.140.factor_r, ...), custom_call_target="tpu_custom_call" | custom-call | flops 1000000 | bytes 1000000 | tf_op jit(solution)/shard_map/update/pallas_call | solution.py:706

commit v2 on v1

--- a/solution.py
+++ b/solution.py
@@ -1,4 +1,5 @@
 import functools
+import math
 
 import jax
 import jax.numpy as jnp
@@ -76,19 +77,28 @@
 
 
 class Sum:
-    PHASES = 5
-
-    def __init__(self, place, refs, out, square, scratch):
-        self.place, self.refs, self.out, self.square = place, refs, out, square
-        self.kept, self.got, self.far, self.got_x, self.near, self.got_1, self.pair, self.got_2, self.local, self.send, self.recv = scratch
-        half = self.far.shape[0] // 2
+    FIRST = {"all": 0, "x": 0, "yz": 2}
+    LAST = {"all": 4, "x": 2, "yz": 4}
+
+    def __init__(self, place, kind, refs, outs, scratch):
+        self.place, self.kind, self.refs, self.out = place, kind, refs, outs[0]
+        self.square = outs[1] if kind != "x" else None
+        self.local, self.send, self.recv = scratch[-3:]
+        scratch = scratch[:-3]
+        if kind != "yz":
+            self.kept, self.got, self.far, self.got_x = scratch[:4]
+            scratch = scratch[4:]
+        if kind != "x":
+            self.near, self.got_1, self.pair, self.got_2 = scratch
+        half = self.out.shape[0] // 2
         self.top, self.low = pl.ds(0, half), pl.ds(half, half)
 
     @staticmethod
-    def scratch(rows, cols):
+    def scratch(kind, rows, cols):
         one = lambda *lead: pltpu.VMEM((*lead, rows, cols), BF16)
-        sems = [pltpu.SemaphoreType.DMA((k,)) for k in (2, 7, 7)]
-        return [one(2), one(2), one(), one(), one(), one(), one(), one(), *sems]
+        to_x = [one(2), one(2), one(), one()] if kind != "yz" else []
+        to_yz = [one()] * 4 if kind != "x" else []
+        return to_x + to_yz + [pltpu.SemaphoreType.DMA((k,)) for k in (2, 7, 7)]
 
     def copies(self, phase):
         p, over = self.place, lambda i, src, dst, to: remote(src, dst, self.send.at[i], self.recv.at[i], to)
@@ -107,6 +117,8 @@
         ]
 
     def locals(self):
+        if self.kind == "yz":
+            return [pltpu.make_async_copy(self.refs[0], self.near, self.local.at[0])]
         return [pltpu.make_async_copy(self.refs[i], self.kept.at[i], self.local.at[i]) for i in range(2)]
 
     def run(self, phase):
@@ -116,60 +128,99 @@
             for one in self.locals() + self.copies(0):
                 one.start()
             return
-        for one in self.copies(phase - 1):
-            one.wait()
+        if phase == 2 and self.kind == "yz":
+            for one in self.locals():
+                one.start()
+                one.wait()
+        else:
+            for one in self.copies(phase - 1):
+                one.wait()
         if phase == 1:
             for one in self.locals():
                 one.wait()
             self.far[...] = (wide(self.kept[1 - x]) + wide(self.got[1 - x])).astype(BF16)
-        elif phase == 2:
-            self.near[...] = (wide(self.kept[x]) + wide(self.got[x]) + wide(self.got_x[...])).astype(BF16)
+        elif phase == 2 and self.kind != "yz":
+            into = self.out if self.kind == "x" else self.near
+            into[...] = (wide(self.kept[x]) + wide(self.got[x]) + wide(self.got_x[...])).astype(BF16)
         elif phase == 3:
             self.pair[...] = (wide(self.near[...]) + wide(self.got_1[...])).astype(BF16)
-        else:
+        elif phase == 4:
             total = (wide(self.pair[...]) + wide(self.got_2[...])).astype(BF16)
             self.out[...] = total
             self.square[...] = jnp.full(self.square.shape, jnp.sum(wide(total) * wide(total)), F32)
-            return
-        for one in self.copies(phase):
-            one.start()
+        if phase < Sum.LAST[self.kind]:
+            for one in self.copies(phase):
+                one.start()
+
+
+def timeline(sizes, kinds, steps, step_us):
+    rate = {"core": 4e5, "x": 4.6e4, "y": 4.6e4, "z": 4.6e4}
+    free = dict.fromkeys(rate, 0.0)
+    parts = {0: (("core", 2.0),), 1: (("x", 1.0),), 2: (("y", 0.5), ("z", 0.5)), 3: (("y", 0.5), ("z", 0.5))}
+    phase = [Sum.FIRST[kind] for kind in kinds]
+    ready, order, now, k = [0.0] * len(sizes), [], 0.0, 0
+    while any(p <= Sum.LAST[kind] for p, kind in zip(phase, kinds)):
+        waiting = [i for i, kind in enumerate(kinds) if phase[i] <= Sum.LAST[kind]]
+        able = [i for i in waiting if ready[i] <= now]
+        if not able and k < steps:
+            k += 1
+            now = max(now, k * step_us)
+            continue
+        i = min(able or waiting, key=lambda j: (ready[j], -phase[j], j))
+        now = max(now, ready[i])
+        order.append((k, i, phase[i]))
+        ends = [now]
+        for link, share in parts.get(phase[i], ()):
+            free[link] = max(free[link], now) + share * sizes[i][0] * sizes[i][1] * 2 / rate[link]
+            ends.append(free[link] + 2.0)
+        ready[i] = max(ends)
+        phase[i] += 1
+    return order
 
 
 class Load:
-    def __init__(self, terms, id):
-        self.terms, self.id = terms, id
-        self.sizes = [one[0].shape for one in terms]
-        self.args = [ref for one in terms for ref in one]
+    def __init__(self, id, jobs):
+        self.id = id
+        self.kinds = [kind for kind, _, _ in jobs]
+        self.parts = [part for _, _, part in jobs]
+        self.sizes = [
+            tuple(part[2] if part and part[0] == i else size for i, size in enumerate(terms[0].shape)) for _, terms, part in jobs
+        ]
+        self.counts = [len(terms) for _, terms, _ in jobs]
+        self.args = [ref for _, terms, _ in jobs for ref in terms]
         self.in_specs = [pl.BlockSpec(memory_space=pl.ANY)] * len(self.args)
         here = lambda *_: (0, 0)
-        self.out_specs = [once(size, here) for one in self.sizes for size in (one, (8, 128))]
-        self.out_shape = [shape(size, dtype) for one in self.sizes for size, dtype in ((one, BF16), ((8, 128), F32))]
-        self.scratch = [ref for size in self.sizes for ref in Sum.scratch(*size)]
+        results = [
+            each for size, kind in zip(self.sizes, self.kinds) for each in [(size, BF16)] + ([] if kind == "x" else [((8, 128), F32)])
+        ]
+        self.out_specs = [once(size, here) for size, _ in results]
+        self.out_shape = [shape(size, dtype) for size, dtype in results]
+        self.scratch = [ref for size, kind in zip(self.sizes, self.kinds) for ref in Sum.scratch(kind, *size)]
 
     def sums(self, place, ins, outs, scratch):
-        per = len(scratch) // len(self.sizes)
-        return [
-            Sum(place, ins[4 * i : 4 * i + 4], outs[2 * i], outs[2 * i + 1], scratch[per * i : per * i + per])
-            for i in range(len(self.sizes))
-        ]
-
-    def drive(self, place, sums, step, at):
-        for phase, when in enumerate(at):
-
-            @pl.when(step == when)
-            def _(phase=phase):
-                if phase == 0:
-                    place.meet()
-                for one in sums:
-                    one.run(phase)
+        made = []
+        for kind, part, size, count in zip(self.kinds, self.parts, self.sizes, self.counts):
+            terms, ins = ins[:count], ins[count:]
+            if part is not None:
+                at = pl.ds(*part[1:])
+                terms = [ref.at[at] if part[0] == 0 else ref.at[:, at] for ref in terms]
+            n = 1 if kind == "x" else 2
+            m = len(Sum.scratch(kind, *size))
+            made.append(Sum(place, kind, terms, outs[:n], scratch[:m]))
+            outs, scratch = outs[n:], scratch[m:]
+        return made
 
     def results(self, outs):
-        return list(zip(outs[0::2], outs[1::2]))
-
-
-def carried(body, load, own_in, own_out, at):
-    if load is None:
-        return body
+        made = []
+        for kind in self.kinds:
+            n = 1 if kind == "x" else 2
+            made.append(outs[0] if n == 1 else (outs[0], outs[1]))
+            outs = outs[n:]
+        return made
+
+
+def carried(body, load, own_in, own_out, steps, step_us):
+    order = timeline(load.sizes, load.kinds, steps, step_us)
 
     def both(*refs):
         n_in, n_out, n_scratch = len(load.in_specs), len(load.out_specs), len(load.scratch)
@@ -179,18 +230,34 @@
         more_out, refs = refs[:n_out], refs[n_out:]
         scratch, more_scratch = refs[: len(refs) - n_scratch], refs[len(refs) - n_scratch :]
         place = Place()
-        load.drive(place, load.sums(place, more_in, more_out, more_scratch), pl.program_id(0), at)
+        step = pl.program_id(0)
+        sums = load.sums(place, more_in, more_out, more_scratch)
+
+        def act(at):
+            todo = [(i, phase) for when, i, phase in order if when == at]
+            if todo:
+
+                @pl.when(step == min(at, steps - 1))
+                def _():
+                    if at == 0:
+                        place.meet()
+                    for i, phase in todo:
+                        sums[i].run(phase)
+
+        for at in range(steps):
+            act(at)
         body(*ins, *outs, *scratch)
+        act(steps)
 
     return both
 
 
-def call_with(load, at, body, name, grid, in_specs, out_specs, out_shape, scratch, flops, moved, args):
+def call_with(load, step_us, body, name, grid, in_specs, out_specs, out_shape, scratch, flops, moved, args):
     if load is None:
         outs = call(body, name, grid, in_specs, out_specs, out_shape, scratch, flops, moved)(*args)
         return list(outs), []
     outs = call(
-        carried(body, load, len(in_specs), len(out_specs), at),
+        carried(body, load, len(in_specs), len(out_specs), grid[0], step_us),
         name,
         grid,
         in_specs + load.in_specs,
@@ -229,9 +296,9 @@
 class Fetch:
     COPIES = 9
 
-    def __init__(self, place, own, full, columns, send, recv, local, stage=None):
+    def __init__(self, place, own, full, columns, send, recv, local, stage=None, last="x"):
         self.place, self.own, self.full, self.columns = place, own, full, columns
-        self.send, self.recv, self.local, self.stage = send, recv, local, stage
+        self.send, self.recv, self.local, self.stage, self.last = send, recv, local, stage, last
 
     def part(self, block, quarter=None):
         rows = self.own.shape[0]
@@ -256,23 +323,34 @@
         over = lambda src, dst, to: remote(src, dst, self.send.at[i], self.recv.at[i], to)
         if i == 0:
             return over(self.mine(), self.part(p.s), p.core)
-        if i in (1, 2):
+        if i == 1 or (i == 2 and self.last == "x"):
             q = p.r if i == 1 else p.r_yz
             return over(self.mine(q), self.part(p.s, q), p.over_x)
+        if i == 2:
+            q, to = (p.r_z, p.over_y) if self.last == "y" else (p.r_y, p.over_z)
+            return over(self.part(p.s_x, q), self.part(p.s_x, q), to)
         if i in (3, 4):
             return over(self.part(p.s_x, p.r), self.part(p.s_x, p.r), p.over_y if i == 3 else p.over_z)
         q = (p.r, p.r_yz, p.r_y, p.r_z)[i - 5]
         return over(self.part(p.s_x, q), self.part(p.s_x, q), p.core)
 
+    def received(self, i):
+        p = self.place
+        if i == 0:
+            return self.part(p.s_core)
+        block, q = [(p.s_x, p.r), (p.s_x, p.r_yz), (p.s_x, p.r_y), (p.s_x, p.r_z)][i - 1] if i < 5 else (p.s_both, (p.r, p.r_yz, p.r_y, p.r_z)[i - 5])
+        return self.part(block, q)
+
     def start(self, *which):
         for i in which:
             self.copy(i).start()
 
     def arrived(self, i):
-        self.copy(i).wait_recv()
+        here = self.received(i)
+        remote(here, here, self.send.at[i], self.recv.at[i], self.place.core).wait_recv()
 
     def begin(self):
-        self.start(1, 2, 0)
+        self.start(1, *((2,) if self.last == "x" else ()), 0)
         into = self.stage if self.stage is not None else self.part(self.place.s)
         pltpu.make_async_copy(self.mine(), into, self.local.at[0]).start()
 
@@ -284,12 +362,14 @@
             pltpu.make_async_copy(self.stage, self.part(self.place.s), self.local.at[1]).start()
 
     def hand_over(self):
+        self.arrived(3)
+        self.start(7, *((2,) if self.last == "z" else ()))
+        self.arrived(4)
+        self.start(8, *((2,) if self.last == "y" else ()))
+
+    def hand_last(self):
         self.arrived(2)
         self.start(6)
-        self.arrived(3)
-        self.start(7)
-        self.arrived(4)
-        self.start(8)
 
     def finish(self):
         if self.stage is not None:
@@ -306,72 +386,68 @@
 
 
 def project_body(h_ref, *refs):
-    own, refs = [ref.at[number] for number in range(2) for ref in refs[:3]], refs[3:]
+    g, u, d, refs = *refs[:3], refs[3:]
     gate_ref, up_ref, prod_ref = refs[:3]
-    full, refs = refs[3:7], refs[7:]
-    a_all, wg, wu, stage_d0, stage_g1, stage_u1, stage_d1, send, recv, local = refs
+    full, refs = refs[3:6], refs[6:]
+    a_all, wg, wu, stage_d0, stage_g1, stage_u1, send, recv, local = refs
     run, tile = pl.program_id(0), pl.program_id(1)
     step = run * pl.num_programs(1) + tile
     place = Place()
     ff = wg.shape[1]
     plan = [
-        (own[0], wg, (0, HEAD), None),
-        (own[1], wu, (0, HEAD), None),
-        (own[0], wg, (HEAD, ff - HEAD), None),
-        (own[1], wu, (HEAD, ff - HEAD), None),
-        (own[2], full[0], None, stage_d0),
-        (own[3], full[1], (0, ff), stage_g1),
-        (own[4], full[2], (0, ff), stage_u1),
-        (own[5], full[3], None, stage_d1),
+        (g.at[0], wg, (0, HEAD), None, "x"),
+        (u.at[0], wu, (0, HEAD), None, "x"),
+        (g.at[0], wg, (HEAD, ff - HEAD), None, "x"),
+        (u.at[0], wu, (HEAD, ff - HEAD), None, "x"),
+        (d.at[0], full[0], None, stage_d0, "x"),
+        (g.at[1], full[1], (0, ff), stage_g1, "y"),
+        (u.at[1], full[2], (0, ff), stage_u1, "x"),
     ]
     fetches = [
-        Fetch(place, mine, whole, columns, send.at[i], recv.at[i], local.at[i], stage) for i, (mine, whole, columns, stage) in enumerate(plan)
+        Fetch(place, mine, whole, columns, send.at[i], recv.at[i], local.at[i], stage, last)
+        for i, (mine, whole, columns, stage, last) in enumerate(plan)
     ]
+
+    def act(moves):
+        for when, number, what in moves:
+
+            @pl.when(step == when)
+            def _(number=number, what=what):
+                getattr(fetches[number], what)()
 
     @pl.when(step == 0)
     def _():
         place.meet()
         a, b, c, d = fetches[:4]
-        for one in (a, b):
+        for one in (a, b, c, d):
             one.begin()
-        for one in (c, d):
-            one.begin()
-        for one in (a, b):
-            one.relay()
-        for one in (a, b):
-            one.hand_over()
-        for one in (a, b):
-            one.finish()
-
-    for when, number, what in (
-        (1, 2, "relay"),
-        (1, 3, "relay"),
-        (1, 4, "begin"),
-        (3, 2, "hand_over"),
-        (3, 3, "hand_over"),
-        (4, 4, "relay"),
-        (4, 5, "begin"),
-        (5, 4, "hand_over"),
-        (7, 2, "finish"),
-        (7, 3, "finish"),
-        (8, 5, "relay"),
-        (8, 6, "begin"),
-        (10, 4, "finish"),
-        (11, 5, "hand_over"),
-        (11, 6, "relay"),
-        (11, 7, "begin"),
-        (14, 6, "hand_over"),
-        (14, 7, "relay"),
-        (17, 7, "hand_over"),
-        (18, 5, "finish"),
-        (18, 6, "finish"),
-        (19, 7, "finish"),
-    ):
-
-        @pl.when(step == when)
-        def _(number=number, what=what):
-            getattr(fetches[number], what)()
-
+        for what in ("relay", "hand_over", "hand_last", "finish"):
+            for one in (a, b):
+                getattr(one, what)()
+
+    act(
+        (
+            (1, 2, "relay"),
+            (4, 3, "relay"),
+            (4, 2, "hand_over"),
+            (4, 2, "hand_last"),
+            (4, 4, "begin"),
+            (6, 3, "hand_over"),
+            (6, 3, "hand_last"),
+            (6, 5, "begin"),
+            (7, 2, "finish"),
+            (7, 3, "finish"),
+            (8, 4, "relay"),
+            (8, 6, "begin"),
+            (11, 4, "hand_over"),
+            (11, 4, "hand_last"),
+            (12, 5, "relay"),
+            (14, 4, "finish"),
+            (15, 5, "hand_over"),
+            (15, 6, "relay"),
+            (18, 5, "hand_last"),
+        )
+    )
     rows = h_ref.shape[0]
     mine = pl.ds(pl.multiple_of(tile * rows, rows), rows)
 
@@ -380,18 +456,26 @@
         a_all[mine, :] = normed(h_ref[...])
 
     a = a_all[mine, :]
-    across = pl.ds(pl.multiple_of(run * RUN, RUN), RUN)
-    gate = dot(a, wg[:, across], NN)
-    up = dot(a, wu[:, across], NN)
-    gate_ref[...] = gate
-    up_ref[...] = up
-    prod_ref[...] = (gate * jax.nn.sigmoid(gate) * up).astype(BF16)
+    part = RUN // 2
+    front = lambda i: [
+        dot(a, w[:, pl.ds(pl.multiple_of(run * RUN + i * part, part), part)], NN) for w in (wg, wu)
+    ]
+    ahead = front(0)
+    for i in range(2):
+        gate, up = ahead
+        if i == 0:
+            ahead = front(1)
+        at = slice(i * part, (i + 1) * part)
+        gate_ref[:, at] = gate
+        up_ref[:, at] = up
+        prod_ref[:, at] = (gate * jax.nn.sigmoid(gate) * up).astype(BF16)
+    act(((19, 6, "hand_over"), (19, 6, "hand_last"), (19, 5, "finish"), (19, 6, "finish")))
 
 
 def project(h, weights, tile=1024):
     n, d = h.shape
     ff = weights[0].shape[2]
-    sizes = [one.shape[1:] for one in (weights[2], *weights)]
+    sizes = [one.shape[1:] for one in (weights[2], *weights[:2])]
     rows = pl.BlockSpec((tile, RUN), lambda i, j: (j, i))
     hbm = pl.BlockSpec(memory_space=pl.ANY)
     outs = call(
@@ -399,12 +483,12 @@
         "project",
         (ff // RUN, n // tile),
         [pl.BlockSpec((tile, d), lambda i, j: (jnp.where(i == 0, j, n // tile - 1), 0))] + [hbm] * 3,
-        [rows] * 3 + [hbm] * 4,
+        [rows] * 3 + [hbm] * 3,
         [shape((n, ff), F32), shape((n, ff), F32), shape((n, ff), BF16)]
-        + [shape((rows_ * 4, cols), BF16) for rows_, cols in sizes],
+        + [shape((high * 4, cols), BF16) for high, cols in sizes],
         [pltpu.VMEM((n, d), BF16), pltpu.VMEM((d, ff), BF16), pltpu.VMEM((d, ff), BF16)]
         + [pltpu.VMEM(size, BF16) for size in sizes]
-        + [pltpu.SemaphoreType.DMA((8, 9)), pltpu.SemaphoreType.DMA((8, 9)), pltpu.SemaphoreType.DMA((8, 2))],
+        + [pltpu.SemaphoreType.DMA((7, 9)), pltpu.SemaphoreType.DMA((7, 9)), pltpu.SemaphoreType.DMA((7, 2))],
         4 * n * d * ff,
         n * ff * 10,
         0,
@@ -412,25 +496,43 @@
     return outs[:3], outs[3:]
 
 
-def down_body(h_ref, prod_ref, wd_ref, out_ref):
+def down_body(h_ref, prod_ref, wd_ref, d_ref, out_ref, full, stage, send, recv, local):
+    step = pl.program_id(0)
+    place = Place()
+    fetch = Fetch(place, d_ref.at[1], full, None, send, recv, local, stage)
+
+    def act(when, *what):
+        @pl.when(step == when)
+        def _():
+            if when == 0:
+                place.meet()
+            for one in what:
+                getattr(fetch, one)()
+
+    act(0, "begin")
+    act(3, "relay")
+    act(5, "hand_over", "hand_last")
     out_ref[...] = h_ref[...] + dot(prod_ref[...], wd_ref[...], NN).astype(BF16)
-
-
-def down(h, prod, wd, tile=512):
+    act(pl.num_programs(0) - 1, "finish")
+
+
+def down(h, prod, wd, w_down, tile=512):
     n, d = h.shape
     ff = wd.shape[0]
     rows = lambda width: pl.BlockSpec((tile, width), lambda i: (i, 0))
+    hbm = pl.BlockSpec(memory_space=pl.ANY)
     return call(
         down_body,
         "down",
         (n // tile,),
-        [rows(d), rows(ff), once((ff, d), lambda i: (0, 0))],
-        rows(d),
-        shape((n, d), BF16),
-        [],
+        [rows(d), rows(ff), once((ff, d), lambda i: (0, 0)), hbm],
+        [rows(d), hbm],
+        [shape((n, d), BF16), shape((ff, d), BF16)],
+        [pltpu.VMEM(w_down.shape[1:], BF16), pltpu.SemaphoreType.DMA((9,)), pltpu.SemaphoreType.DMA((9,)), pltpu.SemaphoreType.DMA((2,))],
         2 * n * d * ff,
         n * ff * 2,
-    )(h, prod, wd)
+        7,
+    )(h, prod, wd, w_down)
 
 
 def slopes(gate, up, dprod):
@@ -471,14 +573,14 @@
             ref[...] = acc_d[:, pl.ds(pl.multiple_of(core * rows, rows), rows)].T.astype(BF16)
 
 
-def last(h, dy, wg, wu, wd, run, runs, load=None, at=(), tile=256, part=256):
+def last(h, dy, wg, wu, wd, run, runs, load=None, step_us=1.0, tile=512, part=256):
     n, d = h.shape
     ff = wg.shape[1] // runs
     rows = lambda width: pl.BlockSpec((tile, width), lambda i: (i, 0))
     columns = lambda: once((d, ff), lambda i: (0, run))
     outs, done = call_with(
         load,
-        at,
+        step_us,
         functools.partial(last_body, part),
         f"last{run}",
         (n // tile,),
@@ -505,14 +607,14 @@
     out_ref[...] = by_ref[...] + dh.astype(BF16)
 
 
-def inward(h, by, dgates, dups, wg, wu, load=None, at=(), tile=512):
+def inward(h, by, dgates, dups, wg, wu, load=None, step_us=1.0, tile=512):
     n, d = h.shape
     ff = wg.shape[1]
     runs = len(dgates)
     rows = lambda width: pl.BlockSpec((tile, width), lambda i: (i, 0))
     outs, done = call_with(
         load,
-        at,
+        step_us,
         functools.partial(inward_body, runs),
         "inward",
         (n // tile,),
@@ -542,13 +644,13 @@
             ref[...] = acc[:, pl.ds(pl.multiple_of(block * rows, rows), rows)].T.astype(BF16)
 
 
-def outer(by, prod, load=None, at=(), tile=512):
+def outer(by, prod, load=None, step_us=1.0, tile=512):
     n, d = by.shape
     ff = prod.shape[1]
     rows = lambda width: pl.BlockSpec((tile, width), lambda i: (i, 0))
     return call_with(
         load,
-        at,
+        step_us,
         outer_body,
         "outer",
         (n // tile,),
@@ -562,22 +664,25 @@
     )
 
 
-def first_body(part, h_ref, by_ref, gate_ref, up_ref, wd_ref, *rest):
+def first_body(part, blocks, h_ref, by_ref, *rest):
+    gates, ups, wds, rest = rest[:blocks], rest[blocks : 2 * blocks], rest[2 * blocks : 3 * blocks], rest[3 * blocks :]
     outs, (acc_g, acc_u) = rest[:8], rest[8:]
     step = pl.program_id(0)
     clear(step, acc_g, acc_u)
     a_t = normed(h_ref[...]).T
     by = by_ref[...]
-    parts = [slice(i, i + part) for i in range(0, wd_ref.shape[0], part)]
-    front = lambda at: dot(by, wd_ref[at, :], NT)
-    ahead = front(parts[0])
-    for i, at in enumerate(parts):
+    width = wds[0].shape[0]
+    parts = [(k, slice(i, i + part)) for k in range(blocks) for i in range(0, width, part)]
+    front = lambda k, at: dot(by, wds[k][at, :], NT)
+    ahead = front(*parts[0])
+    for i, (k, at) in enumerate(parts):
         dprod = ahead.astype(BF16).astype(F32)
         if i + 1 < len(parts):
-            ahead = front(parts[i + 1])
-        _, dup, dgate = slopes(gate_ref[:, at], up_ref[:, at], dprod)
-        acc_g[:, at] += dot(a_t, dgate, NN)
-        acc_u[:, at] += dot(a_t, dup, NN)
+            ahead = front(*parts[i + 1])
+        _, dup, dgate = slopes(gates[k][:, at], ups[k][:, at], dprod)
+        to = slice(i * part, (i + 1) * part)
+        acc_g[:, to] += dot(a_t, dgate, NN)
+        acc_u[:, to] += dot(a_t, dup, NN)
 
     @pl.when(step == pl.num_programs(0) - 1)
     def _():
@@ -586,25 +691,28 @@
         spread(acc_u, rows, outs[4:])
 
 
-def first(h, by, gate, up, wd, run, width, load=None, at=(), tile=512, part=256):
+def first(h, by, gate, up, wd, start, width, load=None, step_us=1.0, tile=512, part=256):
     n, d = h.shape
+    block = math.gcd(start, width)
+    blocks = width // block
     rows = lambda: pl.BlockSpec((tile, d), lambda i: (i, 0))
-    kept = lambda: pl.BlockSpec((tile, width), lambda i: (i, run))
+    kept = [pl.BlockSpec((tile, block), lambda i, k=k: (i, start // block + k)) for k in range(blocks)]
+    wds = [once((block, d), lambda i, k=k: (start // block + k, 0)) for k in range(blocks)]
     outs, done = call_with(
         load,
-        at,
-        functools.partial(first_body, part),
-        f"first{run}",
+        step_us,
+        functools.partial(first_body, part, blocks),
+        f"first{start}",
         (n // tile,),
-        [rows(), rows(), kept(), kept(), once((width, d), lambda i: (run, 0))],
+        [rows(), rows()] + kept * 2 + wds,
         spread_specs(d // 4, width, 8),
         spread_shapes(d // 4, width, 8),
         [pltpu.VMEM((d, width), F32)] * 2,
         6 * n * d * width,
         n * width * 8,
-        (h, by, gate, up, wd),
+        (h, by, *[gate] * blocks, *[up] * blocks, *[wd] * blocks),
     )
-    return outs[:4], outs[4:], done
+    return outs[:4], outs[4:8], done
 
 
 def tail_body(count, squares, load, *refs):
@@ -616,13 +724,8 @@
     place = Place()
     sums = load.sums(place, ins, outs, scratch)
     place.meet()
-    for wave in range(len(sums) + Sum.PHASES - 1):
-        for i, one in enumerate(sums):
-            if i == 0 and wave == 0:
-                for each in sums:
-                    each.run(0)
-            if 1 <= wave - i + 1 < Sum.PHASES:
-                one.run(wave - i + 1)
+    for _, i, phase in timeline(load.sizes, load.kinds, 0, 0.0):
+        sums[i].run(phase)
     total = sum(ref[...] for ref in others) + sum(one.square[...] for one in sums)
     mine[...] = total
     hop = remote(mine, got_core, send.at[0], recv.at[0], place.core)
@@ -661,22 +764,21 @@
 
 
 def update_body(edges, factor_ref, *refs):
-    counts = [[len(e) - 1 for e in one] for one in edges]
-    total = sum(map(sum, counts))
+    total = sum(len(edge) - 1 for per_layer in edges for edge in per_layer)
     grads, refs = refs[:total], refs[total:]
     states, news = refs[:9], refs[9:]
-    layer, turn = pl.program_id(0), pl.program_id(1)
+    turn = pl.program_id(0)
     factor = factor_ref[0, 0]
     k = 0
     for i, per_layer in enumerate(edges):
         for number, edge in enumerate(per_layer):
             for low, high in zip(edge, edge[1:]):
 
-                @pl.when((layer == number) & (turn >= low) & (turn < high))
-                def _(ref=grads[k], i=i):
-                    w, m, v = (states[3 * which + i][0] for which in range(3))
+                @pl.when((turn >= low) & (turn < high))
+                def _(ref=grads[k], i=i, number=number):
+                    w, m, v = (states[3 * which + i][number] for which in range(3))
                     for which, one in enumerate(adamw(w.astype(F32), m, v, ref[...].astype(F32) * factor)):
-                        news[3 * which + i][0] = one
+                        news[3 * which + i][number] = one
 
                 k += 1
 
@@ -685,28 +787,28 @@
     specs, edges, args = [pl.BlockSpec(memory_space=pltpu.SMEM)], [], [factor]
     state_specs = []
     for i, per_layer in enumerate(pieces):
-        _, rows, cols = states[i].shape
+        layers, rows, cols = states[i].shape
         tall = i == 2
         block = (rows // turns, cols) if tall else (rows, cols // turns)
         edges.append([])
-        for number, parts in enumerate(per_layer):
+        for parts in per_layer:
             edge = [0]
             for part in parts:
                 low = edge[-1]
                 edge.append(low + (part.shape[0] // block[0] if tall else part.shape[1] // block[1]))
 
-                def index(layer, turn, number=number, low=low, top=edge[-1] - low - 1, tall=tall):
-                    at = jnp.where(layer == number, jnp.clip(turn - low, 0, top), jnp.where(layer < number, 0, top))
+                def index(turn, low=low, top=edge[-1] - low - 1, tall=tall):
+                    at = jnp.clip(turn - low, 0, top)
                     return (at, 0) if tall else (0, at)
 
                 specs.append(pl.BlockSpec(block, index))
                 args.append(part)
             edges[-1].append(edge)
-        state_specs.append(pl.BlockSpec((1, *block), (lambda layer, turn: (layer, turn, 0)) if tall else (lambda layer, turn: (layer, 0, turn))))
+        state_specs.append(pl.BlockSpec((layers, *block), (lambda turn: (0, turn, 0)) if tall else (lambda turn: (0, 0, turn))))
     return call(
         functools.partial(update_body, edges),
         "update",
-        (2, turns),
+        (turns,),
         specs + state_specs * 3,
         state_specs * 3,
         [shape(one.shape, one.dtype) for one in states],
@@ -723,25 +825,30 @@
     def step(x, dy, *arrays):
         weights, m, v = (arrays[i : i + 3] for i in (0, 3, 6))
         h0, dy = x[0], dy[0]
-        (gate, up, prod), (wd0, wg1, wu1, wd1) = project(h0, weights)
-        h1 = down(h0, prod, wd0)
+        (gate, up, prod), (wd0, wg1, wu1) = project(h0, weights)
+        h1, wd1 = down(h0, prod, wd0, weights[2])
         a = last(h1, dy, wg1, wu1, wd1, 0, 2)
-        b = last(h1, dy, wg1, wu1, wd1, 1, 2, Load([a[2], a[3]], 1), (0, 2, 6, 9, 12))
-        (g1a, u1a) = b[5]
-        by, (g1b, u1b) = inward(h1, dy, [a[0], b[0]], [a[1], b[1]], wg1, wu1, Load([b[2], b[3]], 2), (0, 1, 5, 6, 7))
-        d0, (d1,) = outer(by, prod, Load([[a[4][0], b[4][0], a[4][1], b[4][1]]], 3), (0, 1, 5, 6, 7))
-        c = first(h0, by, gate, up, wd0, 0, 1280, Load([d0], 4), (0, 1, 5, 6, 7))
-        (d0,) = c[2]
-        e = first(h0, by, gate, up, wd0, 1, 1280, Load([c[0], c[1]], 5), (0, 1, 5, 6, 7))
-        g0a, u0a = e[2]
-        done = [g1a, u1a, g1b, u1b, d1, d0, g0a, u0a]
+        b = last(h1, dy, wg1, wu1, wd1, 1, 2, Load(1, [("all", a[2], None), ("all", a[3], None)]), 9.0)
+        g1a, u1a = b[5]
+        d1 = [a[4][0], b[4][0], a[4][1], b[4][1]]
+        load = Load(2, [("all", b[2], None), ("all", b[3], None), ("x", d1, None)])
+        by, (g1b, u1b, d1) = inward(h1, dy, [a[0], b[0]], [a[1], b[1]], wg1, wu1, load, 6.4)
+        d0, (d1,) = outer(by, prod, Load(3, [("yz", [d1], None)]), 3.1)
+        halves = lambda terms, cut, by=1: [("all", terms, (by, 0, cut)), ("all", terms, (by, cut, terms[0].shape[by] - cut))]
+        c = first(h0, by, gate, up, wd0, 0, 1536, Load(4, halves(d0, 384, 0)), 7.2)
+        d0 = c[2]
+        load = Load(5, [one for pair in zip(halves(c[0], 768), halves(c[1], 768)) for one in pair])
+        e = first(h0, by, gate, up, wd0, 1536, 1024, load, 4.8)
+        g0a, u0a, g0b, u0b = e[2]
+        done = [g1a, u1a, g1b, u1b, d1, *d0, *e[2]]
         count = ns * sum(w.size for w in weights)
-        (g0b, u0b), factor = tail(Load([e[0], e[1]], 6), [one[1] for one in done], count)
+        load = Load(6, [one for pair in zip(halves(e[0], 512), halves(e[1], 512)) for one in pair])
+        (g0c, u0c, g0d, u0d), factor = tail(load, [one[1] for one in done], count)
         parts = lambda *ones: [one[0] for one in ones]
         pieces = [
-            [parts(g0a, g0b), parts(g1a, g1b)],
-            [parts(u0a, u0b), parts(u1a, u1b)],
-            [parts(d0), parts(d1)],
+            [parts(g0a, g0b, g0c, g0d), parts(g1a, g1b)],
+            [parts(u0a, u0b, u0c, u0d), parts(u1a, u1b)],
+            [parts(*d0), parts(d1)],
         ]
         return tuple(update(factor, pieces, [*weights, *m, *v]))
 

time: 666 us -> 569 us (0.85)
  Pallas kernels: 657 us -> 564 us
    pallas_call x6, Pallas kernels: 405 us -> 331 us  [the longest x5 302 us: call_with(): call(carried(body, load, len(in_specs), len(out_specs), grid[0], step_us)...]
    pallas_call x1, Pallas kernels: 52.9 us -> 40.4 us  [tail(): call(functools.partial(tail_body, count, len(squares), load), 'tail', (),...]
    pallas_call x1, Pallas kernels: 94.2 us -> 84.7 us  [project(): call(project_body, 'project', (ff // RUN, n // tile), [pl.BlockSpec((tile...]
where the time goes in v2:
time: 569 us; the launch traced here: 565 us
  Pallas kernels  564 us (99%)
    pallas_call x5, Pallas kernels, call_with(): call(carried(body, load, len(in_specs), len(out_specs), grid[0], step_us)...  302 us
    pallas_call x1, Pallas kernels, project(): call(project_body, 'project', (ff // RUN, n // tile), [pl.BlockSpec((tile...  84.7 us
    pallas_call x1, Pallas kernels, call_with(): call(body, name, grid, in_specs, out_specs, out_shape, scratch, flops, mo...  76.4 us
    pallas_call x1, Pallas kernels, tail(): call(functools.partial(tail_body, count, len(squares), load), 'tail', (),...  40.4 us
    pallas_call x1, Pallas kernels, down(): call(down_body, 'down', (n // tile,), [rows(d), rows(ff), once((ff, d), l...  31.6 us
    pallas_call x1, Pallas kernels, update(): call(functools.partial(update_body, edges), 'update', (turns,), specs + s...  28.6 us

profile of v2, /device:TPU:0, one launch (start us, length us, event | category | flops | bytes accessed | tf_op | source)
XLA Modules:
  0.0 565.0 jit_solution(4719716789952368351)
XLA Ops:
  0.6 84.7 %project.1 = (f32[4096,2560]{1,0:T(8,128)}, f32[4096,2560]{1,0:T(8,128)}, bf16[4096,2560]{1,0:T(8,128)(2,1)}, bf16[2560,896]{1,0:T(8,128)(2,1)}, bf16[896,2560]{1,0:T(8,128)(2,1)}, /*index=5*/bf16[896,2560]{1,0:T(8,128)(2,1)}) custom-call(bf16[4096,896]{1,0:T(8,128)(2,1)} %bitcast.2, bf16[2,224,2560]{2,1,0:T(8,128)(2,1)} %refs_15_.1, ...), custom_call_target="tpu_custom_call" | custom-call | flops 37580963840 | bytes 104857600 | tf_op jit(solution)/shard_map/project/pallas_call | solution.py:481
  85.4 31.6 %down.1 = (bf16[4096,896]{1,0:T(8,128)(2,1)}, bf16[2560,896]{1,0:T(8,128)(2,1)}) custom-call(bf16[4096,896]{1,0:T(8,128)(2,1)} %bitcast.3, bf16[4096,2560]{1,0:T(8,128)(2,1)} %get-tuple-element.90.prod_ref.refs_1_, bf16[2560,896]{1,0:T(8,128)(2,1)} %get-tuple-element.91.wd_ref.refs_4_.refs_6_.refs_7_, bf16[2,640,896]{2,1,0:T(8,128)(2,1)} %refs_17_.1), custom_call_target="tpu_custom_call" | custom-call | flops 18790481920 | bytes 20971520 | tf_op jit(solution)/shard_map/down/pallas_call | solution.py:524
  117.0 76.4 %last0.1 = (bf16[4096,1280]{1,0:T(8,128)(2,1)}, bf16[4096,1280]{1,0:T(8,128)(2,1)}, bf16[224,1280]{1,0:T(8,128)(2,1)}, bf16[224,1280]{1,0:T(8,128)(2,1)}, bf16[2...) custom-call(bf16[4096,896]{1,0:T(8,128)(2,1)} %get-tuple-element.92., ...), custom_call_target="tpu_custom_call" | custom-call | flops 56371445760 | bytes 20971520 | tf_op jit(solution)/shard_map/last0/pallas_call | solution.py:257
  193.4 81.3 %last1.1 = (bf16[4096,1280]{1,0:T(8,128)(2,1)}, bf16[4096,1280]{1,0:T(8,128)(2,1)}, bf16[224,1280]{1,0:T(8,128)(2,1)}, bf16[224,1280]{1,0:T(8,128)(2,1)}, bf16[2...) custom-call(bf16[4096,896]{1,0:T(8,128)(2,1)} %get-tuple-element.92., ...), custom_call_target="tpu_custom_call" | custom-call | flops 56371445760 | bytes 20971520 | tf_op jit(solution)/shard_map/last1/pallas_call | solution.py:259
  274.7 67.6 %inward.1 = (bf16[4096,896]{1,0:T(8,128)(2,1)}, bf16[224,1280]{1,0:T(8,128)(2,1)}, f32[8,128]{1,0:T(8,128)}, bf16[224,1280]{1,0:T(8,128)(2,1)}, f32[8,128]{1,0:T(8,128)}, /*index=5*/bf16[640,896]{1,0:T(8,128)(2,1)}) custom-call(bf16[4096,896]{1,0:T(8,128)(2,1)} %get-tuple-element.92.h_ref.refs_0_, bf16[4096,896]{1,0:T(8,128)(2,1)} %bitcast.8, ...), custom_call_target="tpu_custom_call" | custom-call | flops 37580963840 | bytes 41943040 | tf_op jit(solution)/shard_map/inward/pallas_call | solution.py:259
  342.3 36.2 %outer.1 = (bf16[640,896]{1,0:T(8,128)(2,1)}, bf16[640,896]{1,0:T(8,128)(2,1)}, bf16[640,896]{1,0:T(8,128)(2,1)}, bf16[640,896]{1,0:T(8,128)(2,1)}, bf16[640,896]{1,0:T(8,128)(2,1)}, /*index=5*/f32[8,128]{1,0:T(8,128)}) custom-call(bf16[4096,896]{1,0:T(8,128)(2,1)} %get-tuple-element.124.refs_0_.refs_1_, ...), custom_call_target="tpu_custom_call" | custom-call | flops 18790481920 | bytes 20971520 | tf_op jit(solution)/shard_map/outer/pallas_call | solution.py:259
  378.6 60.4 %first0.1 = (bf16[224,1536]{1,0:T(8,128)(2,1)}, bf16[224,1536]{1,0:T(8,128)(2,1)}, bf16[224,1536]{1,0:T(8,128)(2,1)}, bf16[224,1536]{1,0:T(8,128)(2,1)}, bf16[22...) custom-call(bf16[4096,896]{1,0:T(8,128)(2,1)} %bitcast.4, ...), custom_call_target="tpu_custom_call" | custom-call | flops 33822867456 | bytes 50331648 | tf_op jit(solution)/shard_map/first0/pallas_call | solution.py:259
  439.0 56.5 %first1536.1 = (bf16[224,1024]{1,0:T(8,128)(2,1)}, bf16[224,1024]{1,0:T(8,128)(2,1)}, bf16[224,1024]{1,0:T(8,128)(2,1)}, bf16[224,1024]{1,0:T(8,128)(2,1)}, bf16...) custom-call(bf16[4096,896]{1,0:T(8,128)(2,1)} %bitcast.5, ...), custom_call_target="tpu_custom_call" | custom-call | flops 22548578304 | bytes 33554432 | tf_op jit(solution)/shard_map/first1536/pallas_call | solution.py:259
  495.5 40.4 %tail.1 = (bf16[224,512]{1,0:T(8,128)(2,1)}, f32[8,128]{1,0:T(8,128)}, bf16[224,512]{1,0:T(8,128)(2,1)}, f32[8,128]{1,0:T(8,128)}, bf16[224,512]{1,0:T(8,128)(2,...) custom-call(f32[8,128]{1,0:T(8,128)} %get-tuple-element.104.refs_0_, ...), custom_call_target="tpu_custom_call" | custom-call | flops 1000 | bytes 1000 | tf_op jit(solution)/shard_map/tail/pallas_call | solution.py:743
  535.9 28.6 %update.1 = (bf16[2,224,2560]{2,1,0:T(8,128)(2,1)}, bf16[2,224,2560]{2,1,0:T(8,128)(2,1)}, bf16[2,640,896]{2,1,0:T(8,128)(2,1)}, f32[2,224,2560]{2,1,0:T(8,128)}...) custom-call(f32[8,128]{1,0:T(8,128)} %get-tuple-element.155.factor_r, ...), custom_call_target="tpu_custom_call" | custom-call | flops 1000000 | bytes 1000000 | tf_op jit(solution)/shard_map/update/pallas_call | solution.py:808

commit v3 on v2

--- a/solution.py
+++ b/solution.py
@@ -219,8 +219,8 @@
         return made
 
 
-def carried(body, load, own_in, own_out, steps, step_us):
-    order = timeline(load.sizes, load.kinds, steps, step_us)
+def carried(body, load, own_in, own_out, steps, step_us, hooks):
+    order = timeline(load.sizes, load.kinds, steps * hooks, step_us / hooks)
 
     def both(*refs):
         n_in, n_out, n_scratch = len(load.in_specs), len(load.out_specs), len(load.scratch)
@@ -237,27 +237,30 @@
             todo = [(i, phase) for when, i, phase in order if when == at]
             if todo:
 
-                @pl.when(step == min(at, steps - 1))
+                @pl.when(step == min(at // hooks, steps - 1))
                 def _():
                     if at == 0:
                         place.meet()
                     for i, phase in todo:
                         sums[i].run(phase)
 
-        for at in range(steps):
-            act(at)
-        body(*ins, *outs, *scratch)
-        act(steps)
+        def pause(now):
+            for at in range(now, steps * hooks, hooks):
+                act(at)
+
+        pause(0)
+        body(*ins, *outs, *scratch, **({"pause": pause} if hooks > 1 else {}))
+        act(steps * hooks)
 
     return both
 
 
-def call_with(load, step_us, body, name, grid, in_specs, out_specs, out_shape, scratch, flops, moved, args):
+def call_with(load, step_us, hooks, body, name, grid, in_specs, out_specs, out_shape, scratch, flops, moved, args):
     if load is None:
         outs = call(body, name, grid, in_specs, out_specs, out_shape, scratch, flops, moved)(*args)
         return list(outs), []
     outs = call(
-        carried(body, load, len(in_specs), len(out_specs), grid[0], step_us),
+        carried(body, load, len(in_specs), len(out_specs), grid[0], step_us, hooks),
         name,
         grid,
         in_specs + load.in_specs,
@@ -296,9 +299,9 @@
 class Fetch:
     COPIES = 9
 
-    def __init__(self, place, own, full, columns, send, recv, local, stage=None, last="x"):
+    def __init__(self, place, own, full, columns, send, recv, local, stage=None):
         self.place, self.own, self.full, self.columns = place, own, full, columns
-        self.send, self.recv, self.local, self.stage, self.last = send, recv, local, stage, last
+        self.send, self.recv, self.local, self.stage = send, recv, local, stage
 
     def part(self, block, quarter=None):
         rows = self.own.shape[0]
@@ -323,12 +326,9 @@
         over = lambda src, dst, to: remote(src, dst, self.send.at[i], self.recv.at[i], to)
         if i == 0:
             return over(self.mine(), self.part(p.s), p.core)
-        if i == 1 or (i == 2 and self.last == "x"):
+        if i in (1, 2):
             q = p.r if i == 1 else p.r_yz
             return over(self.mine(q), self.part(p.s, q), p.over_x)
-        if i == 2:
-            q, to = (p.r_z, p.over_y) if self.last == "y" else (p.r_y, p.over_z)
-            return over(self.part(p.s_x, q), self.part(p.s_x, q), to)
         if i in (3, 4):
             return over(self.part(p.s_x, p.r), self.part(p.s_x, p.r), p.over_y if i == 3 else p.over_z)
         q = (p.r, p.r_yz, p.r_y, p.r_z)[i - 5]
@@ -350,9 +350,12 @@
         remote(here, here, self.send.at[i], self.recv.at[i], self.place.core).wait_recv()
 
     def begin(self):
-        self.start(1, *((2,) if self.last == "x" else ()), 0)
+        self.start(1, 0)
         into = self.stage if self.stage is not None else self.part(self.place.s)
         pltpu.make_async_copy(self.mine(), into, self.local.at[0]).start()
+
+    def begin_last(self):
+        self.start(2)
 
     def relay(self):
         self.arrived(1)
@@ -363,9 +366,9 @@
 
     def hand_over(self):
         self.arrived(3)
-        self.start(7, *((2,) if self.last == "z" else ()))
+        self.start(7)
         self.arrived(4)
-        self.start(8, *((2,) if self.last == "y" else ()))
+        self.start(8)
 
     def hand_last(self):
         self.arrived(2)
@@ -382,72 +385,46 @@
             self.copy(i).wait_send()
 
 
-RUN, HEAD = 512, 1024
+RUN = 512
 
 
 def project_body(h_ref, *refs):
     g, u, d, refs = *refs[:3], refs[3:]
     gate_ref, up_ref, prod_ref = refs[:3]
-    full, refs = refs[3:6], refs[6:]
-    a_all, wg, wu, stage_d0, stage_g1, stage_u1, send, recv, local = refs
+    full, refs = refs[3:5], refs[5:]
+    a_all, wg, wu, stage_d0, stage_g1, send, recv, local = refs
     run, tile = pl.program_id(0), pl.program_id(1)
     step = run * pl.num_programs(1) + tile
     place = Place()
     ff = wg.shape[1]
-    plan = [
-        (g.at[0], wg, (0, HEAD), None, "x"),
-        (u.at[0], wu, (0, HEAD), None, "x"),
-        (g.at[0], wg, (HEAD, ff - HEAD), None, "x"),
-        (u.at[0], wu, (HEAD, ff - HEAD), None, "x"),
-        (d.at[0], full[0], None, stage_d0, "x"),
-        (g.at[1], full[1], (0, ff), stage_g1, "y"),
-        (u.at[1], full[2], (0, ff), stage_u1, "x"),
+    plan = [(own.at[0], whole, across, None) for across in ((0, 512), (512, 1024), (1536, 1024)) for own, whole in ((g, wg), (u, wu))]
+    plan += [(d.at[0], full[0], None, stage_d0), (g.at[1], full[1], (0, ff), stage_g1)]
+    fetches = [
+        Fetch(place, mine, whole, columns, send.at[i], recv.at[i], local.at[i], stage) for i, (mine, whole, columns, stage) in enumerate(plan)
     ]
-    fetches = [
-        Fetch(place, mine, whole, columns, send.at[i], recv.at[i], local.at[i], stage, last)
-        for i, (mine, whole, columns, stage, last) in enumerate(plan)
-    ]
-
-    def act(moves):
-        for when, number, what in moves:
-
-            @pl.when(step == when)
-            def _(number=number, what=what):
-                getattr(fetches[number], what)()
+
+    def act(when, *moves):
+        @pl.when(step == when)
+        def _():
+            for numbers, *what in moves:
+                for each in what:
+                    for number in numbers:
+                        getattr(fetches[number], each)()
 
     @pl.when(step == 0)
     def _():
         place.meet()
-        a, b, c, d = fetches[:4]
-        for one in (a, b, c, d):
-            one.begin()
-        for what in ("relay", "hand_over", "hand_last", "finish"):
-            for one in (a, b):
-                getattr(one, what)()
-
-    act(
-        (
-            (1, 2, "relay"),
-            (4, 3, "relay"),
-            (4, 2, "hand_over"),
-            (4, 2, "hand_last"),
-            (4, 4, "begin"),
-            (6, 3, "hand_over"),
-            (6, 3, "hand_last"),
-            (6, 5, "begin"),
-            (7, 2, "finish"),
-            (7, 3, "finish"),
-            (8, 4, "relay"),
-            (8, 6, "begin"),
-            (11, 4, "hand_over"),
-            (11, 4, "hand_last"),
-            (12, 5, "relay"),
-            (14, 4, "finish"),
-            (15, 5, "hand_over"),
-            (15, 6, "relay"),
-            (18, 5, "hand_last"),
-        )
-    )
+
+    a, b, c, d0, g1 = (0, 1), (2, 3), (4, 5), (6,), (7,)
+    act(0, (a, "begin", "begin_last"), (b, "begin", "begin_last"), (a, "relay", "hand_over", "hand_last", "finish"))
+    act(1, (b, "relay"), (c, "begin", "begin_last"))
+    act(4, (b, "hand_over", "hand_last", "finish"), (d0, "begin", "begin_last"))
+    act(6, (c, "relay"))
+    act(8, (g1, "begin", "begin_last"))
+    act(9, (c, "hand_over", "hand_last"))
+    act(11, (c, "finish"), (d0, "relay"))
+    act(14, (d0, "hand_over", "hand_last"))
+    act(16, (g1, "relay"))
     rows = h_ref.shape[0]
     mine = pl.ds(pl.multiple_of(tile * rows, rows), rows)
 
@@ -469,13 +446,13 @@
         gate_ref[:, at] = gate
         up_ref[:, at] = up
         prod_ref[:, at] = (gate * jax.nn.sigmoid(gate) * up).astype(BF16)
-    act(((19, 6, "hand_over"), (19, 6, "hand_last"), (19, 5, "finish"), (19, 6, "finish")))
+    act(19, (g1, "hand_over", "hand_last"), (d0, "finish"), (g1, "finish"))
 
 
 def project(h, weights, tile=1024):
     n, d = h.shape
     ff = weights[0].shape[2]
-    sizes = [one.shape[1:] for one in (weights[2], *weights[:2])]
+    sizes = [one.shape[1:] for one in (weights[2], weights[0])]
     rows = pl.BlockSpec((tile, RUN), lambda i, j: (j, i))
     hbm = pl.BlockSpec(memory_space=pl.ANY)
     outs = call(
@@ -483,12 +460,12 @@
         "project",
         (ff // RUN, n // tile),
         [pl.BlockSpec((tile, d), lambda i, j: (jnp.where(i == 0, j, n // tile - 1), 0))] + [hbm] * 3,
-        [rows] * 3 + [hbm] * 3,
+        [rows] * 3 + [hbm] * 2,
         [shape((n, ff), F32), shape((n, ff), F32), shape((n, ff), BF16)]
         + [shape((high * 4, cols), BF16) for high, cols in sizes],
         [pltpu.VMEM((n, d), BF16), pltpu.VMEM((d, ff), BF16), pltpu.VMEM((d, ff), BF16)]
         + [pltpu.VMEM(size, BF16) for size in sizes]
-        + [pltpu.SemaphoreType.DMA((7, 9)), pltpu.SemaphoreType.DMA((7, 9)), pltpu.SemaphoreType.DMA((7, 2))],
+        + [pltpu.SemaphoreType.DMA((8, 9)), pltpu.SemaphoreType.DMA((8, 9)), pltpu.SemaphoreType.DMA((8, 2))],
         4 * n * d * ff,
         n * ff * 10,
         0,
@@ -496,27 +473,33 @@
     return outs[:3], outs[3:]
 
 
-def down_body(h_ref, prod_ref, wd_ref, d_ref, out_ref, full, stage, send, recv, local):
+def down_body(h_ref, prod_ref, wd_ref, u_ref, d_ref, out_ref, full_u, full_d, stage_u, stage_d, send, recv, local):
     step = pl.program_id(0)
     place = Place()
-    fetch = Fetch(place, d_ref.at[1], full, None, send, recv, local, stage)
-
-    def act(when, *what):
+    plan = [(u_ref.at[1], full_u, (0, u_ref.shape[2]), stage_u), (d_ref.at[1], full_d, None, stage_d)]
+    fetches = [
+        Fetch(place, mine, whole, columns, send.at[i], recv.at[i], local.at[i], stage) for i, (mine, whole, columns, stage) in enumerate(plan)
+    ]
+
+    def act(when, *moves):
         @pl.when(step == when)
         def _():
             if when == 0:
                 place.meet()
-            for one in what:
-                getattr(fetch, one)()
-
-    act(0, "begin")
-    act(3, "relay")
-    act(5, "hand_over", "hand_last")
+            for numbers, *what in moves:
+                for each in what:
+                    for number in numbers:
+                        getattr(fetches[number], each)()
+
+    act(0, ((0, 1), "begin", "begin_last"))
+    act(3, ((0,), "relay"))
+    act(5, ((1,), "relay"))
+    act(6, ((0,), "hand_over"))
     out_ref[...] = h_ref[...] + dot(prod_ref[...], wd_ref[...], NN).astype(BF16)
-    act(pl.num_programs(0) - 1, "finish")
-
-
-def down(h, prod, wd, w_down, tile=512):
+    act(pl.num_programs(0) - 1, ((0,), "hand_last"), ((1,), "hand_over", "hand_last"), ((0, 1), "finish"))
+
+
+def down(h, prod, wd, w_up, w_down, tile=512):
     n, d = h.shape
     ff = wd.shape[0]
     rows = lambda width: pl.BlockSpec((tile, width), lambda i: (i, 0))
@@ -525,14 +508,15 @@
         down_body,
         "down",
         (n // tile,),
-        [rows(d), rows(ff), once((ff, d), lambda i: (0, 0)), hbm],
-        [rows(d), hbm],
-        [shape((n, d), BF16), shape((ff, d), BF16)],
-        [pltpu.VMEM(w_down.shape[1:], BF16), pltpu.SemaphoreType.DMA((9,)), pltpu.SemaphoreType.DMA((9,)), pltpu.SemaphoreType.DMA((2,))],
+        [rows(d), rows(ff), once((ff, d), lambda i: (0, 0)), hbm, hbm],
+        [rows(d), hbm, hbm],
+        [shape((n, d), BF16), shape((d, ff), BF16), shape((ff, d), BF16)],
+        [pltpu.VMEM(one.shape[1:], BF16) for one in (w_up, w_down)]
+        + [pltpu.SemaphoreType.DMA((2, 9)), pltpu.SemaphoreType.DMA((2, 9)), pltpu.SemaphoreType.DMA((2, 2))],
         2 * n * d * ff,
         n * ff * 2,
         7,
-    )(h, prod, wd, w_down)
+    )(h, prod, wd, w_up, w_down)
 
 
 def slopes(gate, up, dprod):
@@ -581,6 +565,7 @@
     outs, done = call_with(
         load,
         step_us,
+        1,
         functools.partial(last_body, part),
         f"last{run}",
         (n // tile,),
@@ -595,11 +580,13 @@
     return outs[0], outs[1], outs[2:6], outs[6:10], outs[10:12], done
 
 
-def inward_body(runs, h_ref, by_ref, *rest):
+def inward_body(runs, h_ref, by_ref, *rest, pause):
     dgates, dups, (wg_ref, wu_ref, out_ref) = rest[:runs], rest[runs : 2 * runs], rest[2 * runs :]
     ff = dgates[0].shape[1]
     total = lambda parts, w: sum(dot(p[...], w[:, i * ff : (i + 1) * ff], NT) for i, p in enumerate(parts)).astype(BF16)
-    da = (total(dgates, wg_ref) + total(dups, wu_ref)).astype(F32)
+    da = total(dgates, wg_ref)
+    pause(1)
+    da = (da + total(dups, wu_ref)).astype(F32)
     wide = h_ref[...].astype(F32)
     scale = lax.rsqrt(jnp.mean(wide * wide, -1, keepdims=True) + 1e-6)
     along = jnp.mean(da * wide, -1, keepdims=True)
@@ -615,6 +602,7 @@
     outs, done = call_with(
         load,
         step_us,
+        2,
         functools.partial(inward_body, runs),
         "inward",
         (n // tile,),
@@ -651,6 +639,7 @@
     return call_with(
         load,
         step_us,
+        1,
         outer_body,
         "outer",
         (n // tile,),
@@ -664,7 +653,7 @@
     )
 
 
-def first_body(part, blocks, h_ref, by_ref, *rest):
+def first_body(part, blocks, h_ref, by_ref, *rest, pause):
     gates, ups, wds, rest = rest[:blocks], rest[blocks : 2 * blocks], rest[2 * blocks : 3 * blocks], rest[3 * blocks :]
     outs, (acc_g, acc_u) = rest[:8], rest[8:]
     step = pl.program_id(0)
@@ -676,6 +665,8 @@
     front = lambda k, at: dot(by, wds[k][at, :], NT)
     ahead = front(*parts[0])
     for i, (k, at) in enumerate(parts):
+        if i == len(parts) // 2:
+            pause(1)
         dprod = ahead.astype(BF16).astype(F32)
         if i + 1 < len(parts):
             ahead = front(*parts[i + 1])
@@ -701,6 +692,7 @@
     outs, done = call_with(
         load,
         step_us,
+        2,
         functools.partial(first_body, part, blocks),
         f"first{start}",
         (n // tile,),
@@ -825,30 +817,33 @@
     def step(x, dy, *arrays):
         weights, m, v = (arrays[i : i + 3] for i in (0, 3, 6))
         h0, dy = x[0], dy[0]
-        (gate, up, prod), (wd0, wg1, wu1) = project(h0, weights)
-        h1, wd1 = down(h0, prod, wd0, weights[2])
+        (gate, up, prod), (wd0, wg1) = project(h0, weights)
+        h1, wu1, wd1 = down(h0, prod, wd0, weights[1], weights[2])
         a = last(h1, dy, wg1, wu1, wd1, 0, 2)
         b = last(h1, dy, wg1, wu1, wd1, 1, 2, Load(1, [("all", a[2], None), ("all", a[3], None)]), 9.0)
         g1a, u1a = b[5]
         d1 = [a[4][0], b[4][0], a[4][1], b[4][1]]
-        load = Load(2, [("all", b[2], None), ("all", b[3], None), ("x", d1, None)])
-        by, (g1b, u1b, d1) = inward(h1, dy, [a[0], b[0]], [a[1], b[1]], wg1, wu1, load, 6.4)
-        d0, (d1,) = outer(by, prod, Load(3, [("yz", [d1], None)]), 3.1)
-        halves = lambda terms, cut, by=1: [("all", terms, (by, 0, cut)), ("all", terms, (by, cut, terms[0].shape[by] - cut))]
-        c = first(h0, by, gate, up, wd0, 0, 1536, Load(4, halves(d0, 384, 0)), 7.2)
-        d0 = c[2]
-        load = Load(5, [one for pair in zip(halves(c[0], 768), halves(c[1], 768)) for one in pair])
-        e = first(h0, by, gate, up, wd0, 1536, 1024, load, 4.8)
-        g0a, u0a, g0b, u0b = e[2]
-        done = [g1a, u1a, g1b, u1b, d1, *d0, *e[2]]
+        high, low = (0, 0, 384), (0, 384, 256)
+        load = Load(2, [("all", b[2], None), ("all", b[3], None), ("x", d1, high)])
+        by, (g1b, u1b, d1a) = inward(h1, dy, [a[0], b[0]], [a[1], b[1]], wg1, wu1, load, 6.2)
+        d0, (d1a, d1b) = outer(by, prod, Load(3, [("yz", [d1a], None), ("x", d1, low)]), 3.1)
+        load = Load(4, [("all", d0, high), ("x", d0, low), ("yz", [d1b], None)])
+        c = first(h0, by, gate, up, wd0, 0, 1536, load, 5.6)
+        d0a, d0b, d1b = c[2]
+        left, right = (1, 0, 768), (1, 768, 768)
+        load = Load(5, [("all", c[0], left), ("all", c[1], left), ("all", c[0], right), ("x", c[1], right), ("yz", [d0b], None)])
+        e = first(h0, by, gate, up, wd0, 1536, 1024, load, 4.0)
+        g0a, u0a, g0b, u0b, d0b = e[2]
+        done = [g1a, u1a, g1b, u1b, d1a, d1b, d0a, d0b, g0a, u0a, g0b]
         count = ns * sum(w.size for w in weights)
-        load = Load(6, [one for pair in zip(halves(e[0], 512), halves(e[1], 512)) for one in pair])
-        (g0c, u0c, g0d, u0d), factor = tail(load, [one[1] for one in done], count)
+        left, right = (1, 0, 512), (1, 512, 512)
+        load = Load(6, [("all", e[0], left), ("all", e[1], left), ("all", e[0], right), ("all", e[1], right), ("yz", [u0b], None)])
+        (g0c, u0c, g0d, u0d, u0b), factor = tail(load, [one[1] for one in done], count)
         parts = lambda *ones: [one[0] for one in ones]
         pieces = [
             [parts(g0a, g0b, g0c, g0d), parts(g1a, g1b)],
             [parts(u0a, u0b, u0c, u0d), parts(u1a, u1b)],
-            [parts(*d0), parts(d1)],
+            [parts(d0a, d0b), parts(d1a, d1b)],
         ]
         return tuple(update(factor, pieces, [*weights, *m, *v]))
 

time: 569 us -> 562 us (0.988)
  Pallas kernels: 564 us -> 557 us
    pallas_call x5, Pallas kernels: 302 us -> 295 us  [call_with(): call(carried(body, load, len(in_specs), len(out_specs), grid[0], step_us,...]
where the time goes in v3:
time: 562 us; the launch traced here: 558 us
  Pallas kernels  557 us (99%)
    pallas_call x5, Pallas kernels, call_with(): call(carried(body, load, len(in_specs), len(out_specs), grid[0], step_us,...  295 us
    pallas_call x1, Pallas kernels, project(): call(project_body, 'project', (ff // RUN, n // tile), [pl.BlockSpec((tile...  80.8 us
    pallas_call x1, Pallas kernels, call_with(): call(body, name, grid, in_specs, out_specs, out_shape, scratch, flops, mo...  76.4 us
    pallas_call x1, Pallas kernels, tail(): call(functools.partial(tail_body, count, len(squares), load), 'tail', (),...  42.1 us
    pallas_call x1, Pallas kernels, down(): call(down_body, 'down', (n // tile,), [rows(d), rows(ff), once((ff, d), l...  33.4 us
    pallas_call x1, Pallas kernels, update(): call(functools.partial(update_body, edges), 'update', (turns,), specs + s...  28.9 us

profile of v3, /device:TPU:0, one launch (start us, length us, event | category | flops | bytes accessed | tf_op | source)
XLA Modules:
  0.0 558.0 jit_solution(3397984289316417144)
XLA Ops:
  0.6 80.8 %project.1 = (f32[4096,2560]{1,0:T(8,128)}, f32[4096,2560]{1,0:T(8,128)}, bf16[4096,2560]{1,0:T(8,128)(2,1)}, bf16[2560,896]{1,0:T(8,128)(2,1)}, bf16[896,2560]{1,0:T(8,128)(2,1)}) custom-call(bf16[4096,896]{1,0:T(8,128)(2,1)} %bitcast.2, bf16[2,224,2560]{2,1,0:T(8,128)(2,1)} %refs_16_.1, bf16[2,224,2560]{2,1,0:T(8,128)(2,1)} %refs_17_.1, ...), custom_call_target="tpu_custom_call" | custom-call | flops 37580963840 | bytes 104857600 | tf_op jit(solution)/shard_map/project/pallas_call | solution.py:458
  81.5 33.4 %down.1 = (bf16[4096,896]{1,0:T(8,128)(2,1)}, bf16[896,2560]{1,0:T(8,128)(2,1)}, bf16[2560,896]{1,0:T(8,128)(2,1)}) custom-call(bf16[4096,896]{1,0:T(8,128)(2,1)} %bitcast.3, bf16[4096,2560]{1,0:T(8,128)(2,1)} %get-tuple-element.94.prod_ref.refs_1_, bf16[2560,896]{1,0:T(8,128)(2,1)} %get-tuple-element.95.wd_ref.refs_4_.refs_6_.refs_7_, ...), custom_call_target="tpu_custom_call" | custom-call | flops 18790481920 | bytes 20971520 | tf_op jit(solution)/shard_map/down/pallas_call | solution.py:507
  114.9 76.4 %last0.1 = (bf16[4096,1280]{1,0:T(8,128)(2,1)}, bf16[4096,1280]{1,0:T(8,128)(2,1)}, bf16[224,1280]{1,0:T(8,128)(2,1)}, bf16[224,1280]{1,0:T(8,128)(2,1)}, bf16[2...) custom-call(bf16[4096,896]{1,0:T(8,128)(2,1)} %get-tuple-element.96., ...), custom_call_target="tpu_custom_call" | custom-call | flops 56371445760 | bytes 20971520 | tf_op jit(solution)/shard_map/last0/pallas_call | solution.py:260
  191.3 81.8 %last1.1 = (bf16[4096,1280]{1,0:T(8,128)(2,1)}, bf16[4096,1280]{1,0:T(8,128)(2,1)}, bf16[224,1280]{1,0:T(8,128)(2,1)}, bf16[224,1280]{1,0:T(8,128)(2,1)}, bf16[2...) custom-call(bf16[4096,896]{1,0:T(8,128)(2,1)} %get-tuple-element.96., ...), custom_call_target="tpu_custom_call" | custom-call | flops 56371445760 | bytes 20971520 | tf_op jit(solution)/shard_map/last1/pallas_call | solution.py:262
  273.1 66.1 %inward.1 = (bf16[4096,896]{1,0:T(8,128)(2,1)}, bf16[224,1280]{1,0:T(8,128)(2,1)}, f32[8,128]{1,0:T(8,128)}, bf16[224,1280]{1,0:T(8,128)(2,1)}, f32[8,128]{1,0:T(8,128)}, /*index=5*/bf16[384,896]{1,0:T(8,128)(2,1)}) custom-call(bf16[4096,896]{1,0:T(8,128)(2,1)} %get-tuple-element.96.h_ref.refs_0_, bf16[4096,896]{1,0:T(8,128)(2,1)} %bitcast.8, ...), custom_call_target="tpu_custom_call" | custom-call | flops 37580963840 | bytes 41943040 | tf_op jit(solution)/shard_map/inward/pallas_call | solution.py:262
  339.2 32.0 %outer.1 = (bf16[640,896]{1,0:T(8,128)(2,1)}, bf16[640,896]{1,0:T(8,128)(2,1)}, bf16[640,896]{1,0:T(8,128)(2,1)}, bf16[640,896]{1,0:T(8,128)(2,1)}, bf16[384,896...) custom-call(bf16[4096,896]{1,0:T(8,128)(2,1)} %get-tuple-element.128.refs_0_.refs_1_, ...), custom_call_target="tpu_custom_call" | custom-call | flops 18790481920 | bytes 20971520 | tf_op jit(solution)/shard_map/outer/pallas_call | solution.py:262
  371.2 57.9 %first0.1 = (bf16[224,1536]{1,0:T(8,128)(2,1)}, bf16[224,1536]{1,0:T(8,128)(2,1)}, bf16[224,1536]{1,0:T(8,128)(2,1)}, bf16[224,1536]{1,0:T(8,128)(2,1)}, bf16[22...) custom-call(bf16[4096,896]{1,0:T(8,128)(2,1)} %bitcast.4, ...), custom_call_target="tpu_custom_call" | custom-call | flops 33822867456 | bytes 50331648 | tf_op jit(solution)/shard_map/first0/pallas_call | solution.py:262
  429.1 57.3 %first1536.1 = (bf16[224,1024]{1,0:T(8,128)(2,1)}, bf16[224,1024]{1,0:T(8,128)(2,1)}, bf16[224,1024]{1,0:T(8,128)(2,1)}, bf16[224,1024]{1,0:T(8,128)(2,1)}, bf16...) custom-call(bf16[4096,896]{1,0:T(8,128)(2,1)} %bitcast.5, ...), custom_call_target="tpu_custom_call" | custom-call | flops 22548578304 | bytes 33554432 | tf_op jit(solution)/shard_map/first1536/pallas_call | solution.py:262
  486.4 42.1 %tail.1 = (bf16[224,512]{1,0:T(8,128)(2,1)}, f32[8,128]{1,0:T(8,128)}, bf16[224,512]{1,0:T(8,128)(2,1)}, f32[8,128]{1,0:T(8,128)}, bf16[224,512]{1,0:T(8,128)(2,...) custom-call(f32[8,128]{1,0:T(8,128)} %get-tuple-element.108.refs_0_,, ...), custom_call_target="tpu_custom_call" | custom-call | flops 1000 | bytes 1000 | tf_op jit(solution)/shard_map/tail/pallas_call | solution.py:735
  528.5 28.9 %update.1 = (bf16[2,224,2560]{2,1,0:T(8,128)(2,1)}, bf16[2,224,2560]{2,1,0:T(8,128)(2,1)}, bf16[2,640,896]{2,1,0:T(8,128)(2,1)}, f32[2,224,2560]{2,1,0:T(8,128)}...) custom-call(f32[8,128]{1,0:T(8,128)} %get-tuple-element.162.factor_r, ...), custom_call_target="tpu_custom_call" | custom-call | flops 1000000 | bytes 1000000 | tf_op jit(solution)/shard_map/update/pallas_call | solution.py:800

commit v4 on v3

--- a/solution.py
+++ b/solution.py
@@ -1,5 +1,4 @@
 import functools
-import math
 
 import jax
 import jax.numpy as jnp
@@ -13,6 +12,7 @@
 MESH = pl.DeviceIdType.MESH
 VMEM_LIMIT = 60 * 1024 * 1024
 SMALL = VMEM_LIMIT
+WHOLE = 67043328
 
 
 def dot(a, b, dims):
@@ -77,8 +77,8 @@
 
 
 class Sum:
-    FIRST = {"all": 0, "x": 0, "yz": 2}
-    LAST = {"all": 4, "x": 2, "yz": 4}
+    FIRST = {"all": 0, "here": 0, "x": 0, "yz": 2}
+    LAST = {"all": 4, "here": 4, "x": 2, "yz": 4}
 
     def __init__(self, place, kind, refs, outs, scratch):
         self.place, self.kind, self.refs, self.out = place, kind, refs, outs[0]
@@ -88,7 +88,11 @@
         if kind != "yz":
             self.kept, self.got, self.far, self.got_x = scratch[:4]
             scratch = scratch[4:]
-        if kind != "x":
+        if kind == "here":
+            sent, self.got_1, self.got_2 = scratch
+            self.near, self.pair = sent.at[0], sent.at[1]
+            self.refs = [self.kept.at[0], self.kept.at[1], self.near, self.pair]
+        elif kind != "x":
             self.near, self.got_1, self.pair, self.got_2 = scratch
         half = self.out.shape[0] // 2
         self.top, self.low = pl.ds(0, half), pl.ds(half, half)
@@ -97,7 +101,7 @@
     def scratch(kind, rows, cols):
         one = lambda *lead: pltpu.VMEM((*lead, rows, cols), BF16)
         to_x = [one(2), one(2), one(), one()] if kind != "yz" else []
-        to_yz = [one()] * 4 if kind != "x" else []
+        to_yz = [one(2), one(), one()] if kind == "here" else [one()] * 4 if kind != "x" else []
         return to_x + to_yz + [pltpu.SemaphoreType.DMA((k,)) for k in (2, 7, 7)]
 
     def copies(self, phase):
@@ -117,6 +121,8 @@
         ]
 
     def locals(self):
+        if self.kind == "here":
+            return []
         if self.kind == "yz":
             return [pltpu.make_async_copy(self.refs[0], self.near, self.local.at[0])]
         return [pltpu.make_async_copy(self.refs[i], self.kept.at[i], self.local.at[i]) for i in range(2)]
@@ -153,12 +159,12 @@
                 one.start()
 
 
-def timeline(sizes, kinds, steps, step_us):
+def timeline(sizes, kinds, steps, step_us, release=None):
     rate = {"core": 4e5, "x": 4.6e4, "y": 4.6e4, "z": 4.6e4}
     free = dict.fromkeys(rate, 0.0)
     parts = {0: (("core", 2.0),), 1: (("x", 1.0),), 2: (("y", 0.5), ("z", 0.5)), 3: (("y", 0.5), ("z", 0.5))}
     phase = [Sum.FIRST[kind] for kind in kinds]
-    ready, order, now, k = [0.0] * len(sizes), [], 0.0, 0
+    ready, order, now, k = list(release or [0.0] * len(sizes)), [], 0.0, 0
     while any(p <= Sum.LAST[kind] for p, kind in zip(phase, kinds)):
         waiting = [i for i, kind in enumerate(kinds) if phase[i] <= Sum.LAST[kind]]
         able = [i for i in waiting if ready[i] <= now]
@@ -653,99 +659,101 @@
     )
 
 
-def first_body(part, blocks, h_ref, by_ref, *rest, pause):
-    gates, ups, wds, rest = rest[:blocks], rest[blocks : 2 * blocks], rest[2 * blocks : 3 * blocks], rest[3 * blocks :]
-    outs, (acc_g, acc_u) = rest[:8], rest[8:]
-    step = pl.program_id(0)
-    clear(step, acc_g, acc_u)
+def first_body(part, count, squares, load, runs, tiles, step_us, h_ref, by_ref, gate_ref, up_ref, wd_ref, *refs):
+    n_in, n_out, n_scratch = len(load.in_specs), len(load.out_specs), len(load.scratch)
+    others, refs = refs[:squares], refs[squares:]
+    ins, refs = refs[:n_in], refs[n_in:]
+    outs, refs = refs[:n_out], refs[n_out:]
+    own_outs, factor_ref, refs = refs[: 4 * runs], refs[4 * runs], refs[4 * runs + 1 :]
+    (acc_g, acc_u, mine, got_core, both, got_x, send, recv), refs = refs[:8], refs[8:]
+    scratch, refs = refs[:n_scratch], refs[n_scratch:]
+    run, tile = pl.program_id(0), pl.program_id(1)
+    step = run * tiles + tile
+    place = Place()
+    size = (acc_g.shape[0] // 4, acc_g.shape[1])
+    per = len(Sum.scratch("here", *size))
+    own = [Sum(place, "here", None, own_outs[2 * i : 2 * i + 2], refs[per * i : per * i + per]) for i in range(2 * runs)]
+    sums = load.sums(place, ins, outs, scratch) + own
+    release = [0.0] * len(load.sizes) + [(i // 2 + 1) * tiles * step_us for i in range(2 * runs)]
+    order = timeline(load.sizes + [size] * len(own), load.kinds + ["here"] * len(own), runs * tiles, step_us, release)
+
+    def act(at):
+        todo = [(i, phase) for when, i, phase in order if when == at]
+        if todo:
+
+            @pl.when(step == min(at, runs * tiles - 1))
+            def _():
+                if at == 0:
+                    place.meet()
+                for i, phase in todo:
+                    sums[i].run(phase)
+
+    for at in range(runs * tiles):
+        act(at)
+    clear(tile, acc_g, acc_u)
     a_t = normed(h_ref[...]).T
     by = by_ref[...]
-    width = wds[0].shape[0]
-    parts = [(k, slice(i, i + part)) for k in range(blocks) for i in range(0, width, part)]
-    front = lambda k, at: dot(by, wds[k][at, :], NT)
-    ahead = front(*parts[0])
-    for i, (k, at) in enumerate(parts):
-        if i == len(parts) // 2:
-            pause(1)
+    parts = [slice(i, i + part) for i in range(0, wd_ref.shape[0], part)]
+    front = lambda at: dot(by, wd_ref[at, :], NT)
+    ahead = front(parts[0])
+    for i, at in enumerate(parts):
         dprod = ahead.astype(BF16).astype(F32)
         if i + 1 < len(parts):
-            ahead = front(*parts[i + 1])
-        _, dup, dgate = slopes(gates[k][:, at], ups[k][:, at], dprod)
-        to = slice(i * part, (i + 1) * part)
-        acc_g[:, to] += dot(a_t, dgate, NN)
-        acc_u[:, to] += dot(a_t, dup, NN)
-
-    @pl.when(step == pl.num_programs(0) - 1)
+            ahead = front(parts[i + 1])
+        _, dup, dgate = slopes(gate_ref[:, at], up_ref[:, at], dprod)
+        acc_g[:, at] += dot(a_t, dgate, NN)
+        acc_u[:, at] += dot(a_t, dup, NN)
+
+    for number in range(runs):
+
+        @pl.when(step == number * tiles + tiles - 1)
+        def _(number=number):
+            spread(acc_g, size[0], own[2 * number].refs)
+            spread(acc_u, size[0], own[2 * number + 1].refs)
+
+    act(runs * tiles)
+
+    @pl.when(step == runs * tiles - 1)
     def _():
-        rows = acc_g.shape[0] // 4
-        spread(acc_g, rows, outs[:4])
-        spread(acc_u, rows, outs[4:])
-
-
-def first(h, by, gate, up, wd, start, width, load=None, step_us=1.0, tile=512, part=256):
+        total = sum(ref[...] for ref in others) + sum(one.square[...] for one in sums)
+        mine[...] = total
+        hop = remote(mine, got_core, send.at[0], recv.at[0], place.core)
+        hop.start()
+        hop.wait()
+        both[...] = mine[...] + got_core[...]
+        hop = remote(both, got_x, send.at[1], recv.at[1], place.over_x)
+        hop.start()
+        hop.wait()
+        factor_ref[...] = jnp.minimum(1.0, 0.5 * lax.rsqrt((both[...] + got_x[...]) / count + 1e-30))
+
+
+def first(h, by, gate, up, wd, load, squares, count, step_us, tile=512, part=256):
     n, d = h.shape
-    block = math.gcd(start, width)
-    blocks = width // block
-    rows = lambda: pl.BlockSpec((tile, d), lambda i: (i, 0))
-    kept = [pl.BlockSpec((tile, block), lambda i, k=k: (i, start // block + k)) for k in range(blocks)]
-    wds = [once((block, d), lambda i, k=k: (start // block + k, 0)) for k in range(blocks)]
-    outs, done = call_with(
-        load,
-        step_us,
-        2,
-        functools.partial(first_body, part, blocks),
-        f"first{start}",
-        (n // tile,),
-        [rows(), rows()] + kept * 2 + wds,
-        spread_specs(d // 4, width, 8),
-        spread_shapes(d // 4, width, 8),
-        [pltpu.VMEM((d, width), F32)] * 2,
-        6 * n * d * width,
-        n * width * 8,
-        (h, by, *[gate] * blocks, *[up] * blocks, *[wd] * blocks),
-    )
-    return outs[:4], outs[4:8], done
-
-
-def tail_body(count, squares, load, *refs):
-    n_in, n_out = len(load.in_specs), len(load.out_specs)
-    others, refs = refs[:squares], refs[squares:]
-    ins, refs = refs[:n_in], refs[n_in:]
-    outs, factor_ref, refs = refs[:n_out], refs[n_out], refs[n_out + 1 :]
-    scratch, (mine, got_core, both, got_x, send, recv) = refs[: len(load.scratch)], refs[len(load.scratch) :]
-    place = Place()
-    sums = load.sums(place, ins, outs, scratch)
-    place.meet()
-    for _, i, phase in timeline(load.sizes, load.kinds, 0, 0.0):
-        sums[i].run(phase)
-    total = sum(ref[...] for ref in others) + sum(one.square[...] for one in sums)
-    mine[...] = total
-    hop = remote(mine, got_core, send.at[0], recv.at[0], place.core)
-    hop.start()
-    hop.wait()
-    both[...] = mine[...] + got_core[...]
-    hop = remote(both, got_x, send.at[1], recv.at[1], place.over_x)
-    hop.start()
-    hop.wait()
-    factor_ref[...] = jnp.minimum(1.0, 0.5 * lax.rsqrt((both[...] + got_x[...]) / count + 1e-30))
-
-
-def tail(load, squares, count):
-    whole = pl.BlockSpec((8, 128), lambda: (0, 0))
+    runs, tiles = gate.shape[1] // RUN, n // tile
+    rows = pl.BlockSpec((tile, d), lambda i, j: (j, 0))
+    kept = pl.BlockSpec((tile, RUN), lambda i, j: (j, i))
+    whole = once((8, 128), lambda *_: (0, 0))
+    size = (d // 4, RUN)
     outs = call(
-        functools.partial(tail_body, count, len(squares), load),
-        "tail",
-        (),
-        [whole] * len(squares) + load.in_specs,
-        [pl.BlockSpec(one.block_shape, lambda: (0, 0)) for one in load.out_specs] + [whole],
-        load.out_shape + [shape((8, 128), F32)],
-        load.scratch + [pltpu.VMEM((8, 128), F32)] * 4 + [pltpu.SemaphoreType.DMA((2,))] * 2,
-        1000,
-        1000,
+        functools.partial(first_body, part, count, len(squares), load, runs, tiles, step_us),
+        "first",
+        (runs, tiles),
+        [rows, rows, kept, kept, pl.BlockSpec((RUN, d), lambda i, j: (i, 0))] + [whole] * len(squares) + load.in_specs,
+        load.out_specs + [once(size, lambda *_: (0, 0)), whole] * (2 * runs) + [whole],
+        load.out_shape + [shape(size, BF16), shape((8, 128), F32)] * (2 * runs) + [shape((8, 128), F32)],
+        [pltpu.VMEM((d, RUN), F32)] * 2
+        + [pltpu.VMEM((8, 128), F32)] * 4
+        + [pltpu.SemaphoreType.DMA((2,))] * 2
+        + load.scratch
+        + Sum.scratch("here", *size) * (2 * runs),
+        6 * n * d * gate.shape[1],
+        n * gate.shape[1] * 8,
         load.id,
-        SMALL,
-    )(*squares, *load.args)
-    return load.results(outs[:-1]), outs[-1]
+        limit=WHOLE,
+    )(h, by, gate, up, wd, *squares, *load.args)
+    n_out = len(load.out_specs)
+    own = outs[n_out:-1:2]
+    return own[0::2], own[1::2], load.results(outs[:n_out]), outs[-1]
 
 
 def adamw(w, m, v, g):
@@ -827,22 +835,13 @@
         load = Load(2, [("all", b[2], None), ("all", b[3], None), ("x", d1, high)])
         by, (g1b, u1b, d1a) = inward(h1, dy, [a[0], b[0]], [a[1], b[1]], wg1, wu1, load, 6.2)
         d0, (d1a, d1b) = outer(by, prod, Load(3, [("yz", [d1a], None), ("x", d1, low)]), 3.1)
-        load = Load(4, [("all", d0, high), ("x", d0, low), ("yz", [d1b], None)])
-        c = first(h0, by, gate, up, wd0, 0, 1536, load, 5.6)
-        d0a, d0b, d1b = c[2]
-        left, right = (1, 0, 768), (1, 768, 768)
-        load = Load(5, [("all", c[0], left), ("all", c[1], left), ("all", c[0], right), ("x", c[1], right), ("yz", [d0b], None)])
-        e = first(h0, by, gate, up, wd0, 1536, 1024, load, 4.0)
-        g0a, u0a, g0b, u0b, d0b = e[2]
-        done = [g1a, u1a, g1b, u1b, d1a, d1b, d0a, d0b, g0a, u0a, g0b]
-        count = ns * sum(w.size for w in weights)
-        left, right = (1, 0, 512), (1, 512, 512)
-        load = Load(6, [("all", e[0], left), ("all", e[1], left), ("all", e[0], right), ("all", e[1], right), ("yz", [u0b], None)])
-        (g0c, u0c, g0d, u0d, u0b), factor = tail(load, [one[1] for one in done], count)
+        load = Load(4, [("all", d0, high), ("all", d0, low), ("yz", [d1b], None)])
+        squares = [one[1] for one in (g1a, u1a, g1b, u1b, d1a)]
+        g0, u0, (d0a, d0b, d1b), factor = first(h0, by, gate, up, wd0, load, squares, ns * sum(w.size for w in weights), 1.8)
         parts = lambda *ones: [one[0] for one in ones]
         pieces = [
-            [parts(g0a, g0b, g0c, g0d), parts(g1a, g1b)],
-            [parts(u0a, u0b, u0c, u0d), parts(u1a, u1b)],
+            [g0, parts(g1a, g1b)],
+            [u0, parts(u1a, u1b)],
             [parts(d0a, d0b), parts(d1a, d1b)],
         ]
         return tuple(update(factor, pieces, [*weights, *m, *v]))

time: 562 us -> 539 us (0.959)
  Pallas kernels: 557 us -> 534 us
    pallas_call x5 -> x3, Pallas kernels: 295 us -> 180 us  [call_with(): call(carried(body, load, len(in_specs), len(out_specs), grid[0], step_us,...]
    pallas_call x1, Pallas kernels: 42.1 us -> 134 us  [first(): call(functools.partial(first_body, part, count, len(squares), load, runs,...]
where the time goes in v4:
time: 539 us; the launch traced here: 534 us
  Pallas kernels  534 us (99%)
    pallas_call x3, Pallas kernels, call_with(): call(carried(body, load, len(in_specs), len(out_specs), grid[0], step_us,...  180 us
    pallas_call x1, Pallas kernels, first(): call(functools.partial(first_body, part, count, len(squares), load, runs,...  134 us
    pallas_call x1, Pallas kernels, project(): call(project_body, 'project', (ff // RUN, n // tile), [pl.BlockSpec((tile...  80.9 us
    pallas_call x1, Pallas kernels, call_with(): call(body, name, grid, in_specs, out_specs, out_shape, scratch, flops, mo...  76.7 us
    pallas_call x1, Pallas kernels, down(): call(down_body, 'down', (n // tile,), [rows(d), rows(ff), once((ff, d), l...  33.4 us
    pallas_call x1, Pallas kernels, update(): call(functools.partial(update_body, edges), 'update', (turns,), specs + s...  28.8 us

profile of v4, /device:TPU:0, one launch (start us, length us, event | category | flops | bytes accessed | tf_op | source)
XLA Modules:
  0.0 534.4 jit_solution(12198751253981638227)
XLA Ops:
  0.6 80.9 %project.1 = (f32[4096,2560]{1,0:T(8,128)}, f32[4096,2560]{1,0:T(8,128)}, bf16[4096,2560]{1,0:T(8,128)(2,1)}, bf16[2560,896]{1,0:T(8,128)(2,1)}, bf16[896,2560]{1,0:T(8,128)(2,1)}) custom-call(bf16[4096,896]{1,0:T(8,128)(2,1)} %bitcast.5, bf16[2,224,2560]{2,1,0:T(8,128)(2,1)} %refs_18_.1, bf16[2,224,2560]{2,1,0:T(8,128)(2,1)} %refs_19_.1, ...), custom_call_target="tpu_custom_call" | custom-call | flops 37580963840 | bytes 104857600 | tf_op jit(solution)/shard_map/project/pallas_call | solution.py:464
  81.6 33.4 %down.1 = (bf16[4096,896]{1,0:T(8,128)(2,1)}, bf16[896,2560]{1,0:T(8,128)(2,1)}, bf16[2560,896]{1,0:T(8,128)(2,1)}) custom-call(bf16[4096,896]{1,0:T(8,128)(2,1)} %bitcast.6, bf16[4096,2560]{1,0:T(8,128)(2,1)} %get-tuple-element.72.prod_ref.refs_1_, bf16[2560,896]{1,0:T(8,128)(2,1)} %get-tuple-element.73.wd_ref, bf16[2,224,2560]{2,1,0:T(8,128)(2,1)} %refs_19_.1, ...), custom_call_target="tpu_custom_call" | custom-call | flops 18790481920 | bytes 20971520 | tf_op jit(solution)/shard_map/down/pallas_call | solution.py:513
  115.0 76.7 %last0.1 = (bf16[4096,1280]{1,0:T(8,128)(2,1)}, bf16[4096,1280]{1,0:T(8,128)(2,1)}, bf16[224,1280]{1,0:T(8,128)(2,1)}, bf16[224,1280]{1,0:T(8,128)(2,1)}, bf16[2...) custom-call(bf16[4096,896]{1,0:T(8,128)(2,1)} %get-tuple-element.74., ...), custom_call_target="tpu_custom_call" | custom-call | flops 56371445760 | bytes 20971520 | tf_op jit(solution)/shard_map/last0/pallas_call | solution.py:266
  191.7 81.5 %last1.1 = (bf16[4096,1280]{1,0:T(8,128)(2,1)}, bf16[4096,1280]{1,0:T(8,128)(2,1)}, bf16[224,1280]{1,0:T(8,128)(2,1)}, bf16[224,1280]{1,0:T(8,128)(2,1)}, bf16[2...) custom-call(bf16[4096,896]{1,0:T(8,128)(2,1)} %get-tuple-element.74., ...), custom_call_target="tpu_custom_call" | custom-call | flops 56371445760 | bytes 20971520 | tf_op jit(solution)/shard_map/last1/pallas_call | solution.py:268
  273.2 66.1 %inward.1 = (bf16[4096,896]{1,0:T(8,128)(2,1)}, bf16[224,1280]{1,0:T(8,128)(2,1)}, f32[8,128]{1,0:T(8,128)}, bf16[224,1280]{1,0:T(8,128)(2,1)}, f32[8,128]{1,0:T(8,128)}, /*index=5*/bf16[384,896]{1,0:T(8,128)(2,1)}) custom-call(bf16[4096,896]{1,0:T(8,128)(2,1)} %get-tuple-element.74.h_ref.refs_0_, bf16[4096,896]{1,0:T(8,128)(2,1)} %bitcast.4, ...), custom_call_target="tpu_custom_call" | custom-call | flops 37580963840 | bytes 41943040 | tf_op jit(solution)/shard_map/inward/pallas_call | solution.py:268
  339.4 32.0 %outer.1 = (bf16[640,896]{1,0:T(8,128)(2,1)}, bf16[640,896]{1,0:T(8,128)(2,1)}, bf16[640,896]{1,0:T(8,128)(2,1)}, bf16[640,896]{1,0:T(8,128)(2,1)}, bf16[384,896...) custom-call(bf16[4096,896]{1,0:T(8,128)(2,1)} %get-tuple-element.102.refs_0_.by_ref, ...), custom_call_target="tpu_custom_call" | custom-call | flops 18790481920 | bytes 20971520 | tf_op jit(solution)/shard_map/outer/pallas_call | solution.py:268
  371.4 134.1 %first.1 = (bf16[384,896]{1,0:T(8,128)(2,1)}, f32[8,128]{1,0:T(8,128)}, bf16[256,896]{1,0:T(8,128)(2,1)}, f32[8,128]{1,0:T(8,128)}, bf16[256,896]{1,0:T(8,128)(2...) custom-call(bf16[4096,896]{1,0:T(8,128)(2,1)} %bitcast.7, ...), custom_call_target="tpu_custom_call" | custom-call | flops 56371445760 | bytes 83886080 | tf_op jit(solution)/shard_map/first/pallas_call | solution.py:737
  505.5 28.8 %update.1 = (bf16[2,224,2560]{2,1,0:T(8,128)(2,1)}, bf16[2,224,2560]{2,1,0:T(8,128)(2,1)}, bf16[2,640,896]{2,1,0:T(8,128)(2,1)}, f32[2,224,2560]{2,1,0:T(8,128)}...) custom-call(f32[8,128]{1,0:T(8,128)} %get-tuple-element.116.factor_r, ...), custom_call_target="tpu_custom_call" | custom-call | flops 1000000 | bytes 1000000 | tf_op jit(solution)/shard_map/update/pallas_call | solution.py:808
